TPU v7x, 32 devices: a whole 2x2x4 slice. The times are simulated.
32 devices in a mesh: dp: 16 (over z, y, x), mp: 2 (over core).
Axes of the slice: x: 2, y: 2, z: 4, core: 2. Of those that a mesh axis runs over, the one named last changes fastest.
Arguments:
- belief: bfloat16 [4096, 2652], P('dp'), may hold values from -6 to 6
- target_value: bfloat16 [4096, 1326], P('dp'), may hold values from -6 to 6
- counts: int32 [32], P('dp'), may hold values from 1 to 128, as said below
- w_first: bfloat16 [2652, 1536], P(None, 'mp'), may hold values from -0.125 to 0.125
- w_middle: bfloat16 [1536, 1536], P('mp'), may hold values from -0.15625 to 0.15625
- w_last: bfloat16 [1536, 1326], P(None, 'mp'), may hold values from -0.15625 to 0.15625
Outputs:
- grad_first: float32 [2652, 1536], P(None, ('mp', 'dp'))
- grad_middle: float32 [1536, 1536], P('mp', 'dp')
- grad_last: float32 [1536, 1326], P('dp', 'mp')
Inputs may be any that keep to these rules, and one draw needn't show every extreme that they name: `counts`: rows past a subgame's count in its block are padding with arbitrary values.
All inputs are finite; a program needn't handle non-finite values.
Results may differ from a plain program's by a relative error of at most 0.0089.
Values may be sent and summed in bfloat16 or wider, within the bound.
A program may use at most 192 MiB of HBM per device.

v0:
```python
import functools

import jax
import jax.numpy as jnp
from jax import lax
from jax.experimental import pallas as pl
from jax.experimental.pallas import tpu as pltpu
from jax.sharding import PartitionSpec as P

BLOCK = 128
LANES = 128
MESH = pl.DeviceIdType.MESH


def silu_slope(pre_act):
    sigmoid_of = jax.nn.sigmoid(pre_act)
    return sigmoid_of * (1.0 + pre_act * (1.0 - sigmoid_of))


def pad_to(size, step):
    return -(-size // step) * step


def cut_pieces(shapes, cuts):
    pairs = []
    for which, parts in cuts:
        tiles = shapes[which][-1] // LANES
        bounds = [round(tiles * i / (2 * parts)) * LANES for i in range(2 * parts + 1)]
        for i in range(parts):
            pairs.append(
                tuple(
                    (which, bounds[2 * i + t], bounds[2 * i + t + 1] - bounds[2 * i + t])
                    for t in range(2)
                )
            )
    return pairs


def step_kernel(dims, params, pairs, blocks, *refs):
    n_dp, n_mp = dims
    far = n_dp // 4
    count = len(pairs)
    flat = 2 * count
    counts, loads, outs = refs[0], refs[1:6], refs[6:9]
    refs = refs[9:]
    got1, sum1, got2, sum2, got3 = (refs[k * flat : (k + 1) * flat] for k in range(5))
    refs = refs[5 * flat :]
    held, grads = refs[:5], refs[5:8]
    (
        pre1, act1, slope1_t, part2, other2, pre2, act2, act2_t, slope_last, part_back, other_back,
        slope2, slope2_t, load_sems, swap_send, swap_got,
        sq_send, sq_got, send_sems, got_sems, far_send, far_got, sq_sems,
    ) = refs[8:]
    belief, target, w_first, w_middle, w_last = held
    arrivals = [
        pltpu.make_async_copy(src, dst, load_sems.at[i])
        for i, (src, dst) in enumerate(zip(loads, held))
    ]
    for i in (0, 2, 3, 4, 1):
        arrivals[i].start()

    dp, mp = lax.axis_index("dp"), lax.axis_index("mp")
    low, mid, top = dp % 2, (dp // 2) % 2, dp // 4
    me = dp * n_mp + mp
    total = n_dp * n_mp

    barrier = pltpu.get_barrier_semaphore()

    def greet(j, _):
        other = lax.rem(me + j, total)
        pl.semaphore_signal(
            barrier, inc=1, device_id=(other // n_mp, other % n_mp), device_id_type=MESH
        )
        return 0

    lax.fori_loop(1, total, greet, 0)
    pl.semaphore_wait(barrier, total - 1)

    low_peer = (dp + 1 - 2 * low, mp)
    mid_peer = (dp + 2 - 4 * mid, mp)

    def copy1(p, t):
        which, start, width = pairs[p][t]
        cols = pl.ds(start, width)
        src = (
            grads[which].at[:, :, 1 - low, :, cols]
            if t == 0
            else grads[which].at[:, 1 - mid, :, :, cols]
        )
        k = 2 * p + t
        return pltpu.make_async_remote_copy(
            src, got1[k], send_sems.at[0, k], got_sems.at[0, k],
            device_id=low_peer if t == 0 else mid_peer, device_id_type=MESH,
        )

    def copy2(p, t):
        k = 2 * p + t
        return pltpu.make_async_remote_copy(
            sum1[k].at[:, (1 - mid) if t == 0 else (1 - low)], got2[k],
            send_sems.at[1, k], got_sems.at[1, k],
            device_id=mid_peer if t == 0 else low_peer, device_id_type=MESH,
        )

    def copy3(p, t, j):
        k = 2 * p + t
        goal = lax.rem(top + j, far)
        return pltpu.make_async_remote_copy(
            sum2[k].at[goal], got3[k].at[j - 1], far_send.at[k, j - 1], far_got.at[k, j - 1],
            device_id=(dp + (goal - top) * 4, mp), device_id_type=MESH,
        )

    def add1(p, t):
        which, start, width = pairs[p][t]
        k = 2 * p + t

        def body(i, _):
            z, b = i // 2, i % 2
            own = (
                grads[which][z, b, low, :, start : start + width]
                if t == 0
                else grads[which][z, mid, b, :, start : start + width]
            )
            both = own.astype(jnp.float32) + got1[k][z, b].astype(jnp.float32)
            sum1[k][z, b] = both.astype(jnp.bfloat16)
            return 0

        lax.fori_loop(0, 2 * far, body, 0)

    def add2(p, t):
        k = 2 * p + t
        side = mid if t == 0 else low

        def body(z, _):
            both = sum1[k][z, side].astype(jnp.float32) + got2[k][z].astype(jnp.float32)
            sum2[k][z] = both.astype(jnp.bfloat16)
            return 0

        lax.fori_loop(0, far, body, 0)

    rows, hid = act2.shape
    own_width = w_last.shape[1]
    in_width = belief.shape[1]
    block = hid // blocks

    def swap(side, part, other, i):
        return pltpu.make_async_remote_copy(
            part.at[i], other.at[i], swap_send.at[side, i], swap_got.at[side, i],
            device_id=(dp, 1 - mp), device_id_type=MESH,
        )

    def weight_grad(which, left_t, right, stop, start, width):
        r = grads[which].shape[3]
        real = min(width, stop - start)

        def body(z, _):
            at = pl.multiple_of(z * 4 * r, 16)
            value = jnp.dot(
                left_t[pl.ds(at, 4 * r), :], right[:, start : start + real],
                preferred_element_type=jnp.float32,
            )
            if real < width:
                value = jnp.concatenate(
                    [value, jnp.zeros((4 * r, width - real), jnp.float32)], axis=1
                )
            for b in range(4):
                grads[which][z, b // 2, b % 2, :, start : start + width] = value[
                    b * r : (b + 1) * r
                ].astype(jnp.bfloat16)
            return 0

        lax.fori_loop(0, far, body, 0)

    def pair_grads(p, left_t, right, stop):
        for t in range(2):
            which, start, width = pairs[p][t]
            weight_grad(which, left_t, right, stop, start, width)
            copy1(p, t).start()

    own_hid = act1.shape[1]
    arrivals[0].wait()
    arrivals[2].wait()
    for c in range(0, own_hid, 256):
        value = jnp.dot(
            belief[...], w_first[:, c : c + 256], preferred_element_type=jnp.float32
        )
        pre1[:, c : c + 256] = value
        act1[:, c : c + 256] = jax.nn.silu(value).astype(jnp.bfloat16)
    arrivals[3].wait()
    for i in range(blocks):
        part2[i] = jnp.dot(
            act1[...], w_middle[:, i * block : (i + 1) * block],
            preferred_element_type=jnp.float32,
        )
        swap(0, part2, other2, i).start()
    arrivals[1].wait()
    arrivals[4].wait()
    row = lax.broadcasted_iota(jnp.int32, (rows, 1), 0)
    limit = jnp.full((rows, 1), counts[0], jnp.int32)
    for b in range(1, rows // BLOCK):
        limit = jnp.where(row >= b * BLOCK, counts[b] + b * BLOCK, limit)
    live = jnp.where(row < limit, 1.0, 0.0)
    for i in range(blocks):
        cols = slice(i * block, (i + 1) * block)
        swap(0, part2, other2, i).wait_recv()
        value = part2[i] + other2[i]
        pre2[:, cols] = value
        act = jax.nn.silu(value)
        act2[:, cols] = act.astype(jnp.bfloat16)
        act2_t[cols, :] = act.astype(jnp.bfloat16).T
    wanted = target[:, :own_width].astype(jnp.float32)
    for m in range(1, n_mp):
        wanted = jnp.where(
            mp == m, target[:, m * own_width : (m + 1) * own_width].astype(jnp.float32), wanted
        )
    predicted = jnp.dot(act2[...], w_last[...], preferred_element_type=jnp.float32)
    slope_last[...] = (jnp.clip(predicted - wanted, -1.0, 1.0) * live).astype(jnp.bfloat16)
    for i in range(blocks):
        part_back[i] = lax.dot_general(
            slope_last[...], w_last[i * block : (i + 1) * block, :], (((1,), (1,)), ((), ())),
            preferred_element_type=jnp.float32,
        )
        swap(1, part_back, other_back, i).start()
    for p in range(count):
        if pairs[p][0][0] == 2:
            pair_grads(p, act2_t, slope_last, own_width)
    for i in range(blocks):
        cols = slice(i * block, (i + 1) * block)
        swap(1, part_back, other_back, i).wait_recv()
        value = (part_back[i] + other_back[i]) * silu_slope(pre2[:, cols])
        slope2[:, cols] = value.astype(jnp.bfloat16)
        slope2_t[cols, :] = value.astype(jnp.bfloat16).T
    for p in range(count):
        if pairs[p][0][0] == 1:
            pair_grads(p, slope2_t, act1, own_hid)
    for c in range(0, own_hid, 256):
        back = lax.dot_general(
            slope2[...], w_middle[c : c + 256, :], (((1,), (1,)), ((), ())),
            preferred_element_type=jnp.float32,
        )
        value = back * silu_slope(pre1[:, c : c + 256])
        slope1_t[c : c + 256, :] = value.astype(jnp.bfloat16).T
    for i in range(blocks):
        swap(0, part2, other2, i).wait_send()
        swap(1, part_back, other_back, i).wait_send()

    def first_grads(p):
        if pairs[p][0][0] == 0:
            pair_grads(p, slope1_t, belief, in_width)

    for p in range(min(3, count)):
        first_grads(p)
    for i in range(count + 1):
        if i < count:
            for t in range(2):
                copy1(i, t).wait_recv()
                add1(i, t)
                copy2(i, t).start()
            if i + 3 < count:
                first_grads(i + 3)
        if i >= 1:
            for t in range(2):
                copy2(i - 1, t).wait_recv()
                add2(i - 1, t)
                for j in range(1, far):
                    copy3(i - 1, t, j).start()
    squares = jnp.float32(0.0)
    for p in range(count):
        for t in range(2):
            which, start, width = pairs[p][t]
            k = 2 * p + t
            value = sum2[k][top].astype(jnp.float32)
            for j in range(1, far):
                copy3(p, t, j).wait_recv()
                value = value + got3[k][j - 1].astype(jnp.float32)
            outs[which][:, start : start + width] = value
            squares = squares + jnp.sum(value * value)

    sq_send[...] = jnp.full(sq_send.shape, squares, jnp.float32)

    def share_copy(j):
        other = lax.rem(me + j, total)
        return pltpu.make_async_remote_copy(
            sq_send, sq_got.at[j - 1], sq_sems.at[0], sq_sems.at[1],
            device_id=(other // n_mp, other % n_mp), device_id_type=MESH,
        )

    def share(j, _):
        share_copy(j).start()
        return 0

    lax.fori_loop(1, total, share, 0)
    pltpu.make_async_copy(sq_got, sq_got, sq_sems.at[1]).wait()
    everyone = squares + jnp.sum(sq_got[...]) * (1.0 / (sq_send.shape[0] * sq_send.shape[1]))
    scale = lax.rsqrt(jnp.full((1, LANES), everyone / params + 1e-06, jnp.float32))
    for p in range(count):
        for t in range(2):
            which, start, width = pairs[p][t]
            for c in range(start, start + width, LANES):
                outs[which][:, c : c + LANES] = outs[which][:, c : c + LANES] * scale

    for p in range(count):
        for t in range(2):
            copy1(p, t).wait_send()
            copy2(p, t).wait_send()
            for j in range(1, far):
                copy3(p, t, j).wait_send()
    pltpu.make_async_copy(sq_got, sq_got, sq_sems.at[0]).wait()


def per_device(dims, belief, target_value, counts, w_first, w_middle, w_last):
    n_dp, n_mp = dims
    far = n_dp // 4
    blocks = 3
    rows, (in_width, own_hid) = belief.shape[0], w_first.shape
    hid, own_width = w_last.shape
    params = float(n_mp * (w_first.size + w_middle.size + w_last.size))
    shapes = [
        (far, 2, 2, long // n_dp, pad_to(wide, LANES))
        for long, wide in ((own_hid, in_width), (hid, own_hid), (hid, own_width))
    ]
    pairs = cut_pieces(shapes, ((2, 1), (1, 1), (0, 4)))

    def buffers(lead):
        return [
            pltpu.VMEM(lead + (shapes[piece[0]][3], piece[2]), jnp.bfloat16)
            for pair in pairs
            for piece in pair
        ]

    flat = 2 * len(pairs)
    loads = (belief, target_value, w_first, w_middle, w_last)
    swapped = pltpu.VMEM((blocks, rows, hid // blocks), jnp.float32)
    half, single = jnp.bfloat16, jnp.float32
    first, middle, last = pl.pallas_call(
        functools.partial(step_kernel, dims, params, pairs, blocks),
        out_shape=[jax.ShapeDtypeStruct(s[3:], jnp.float32) for s in shapes],
        in_specs=[pl.BlockSpec(memory_space=pltpu.SMEM)]
        + [pl.BlockSpec(memory_space=pl.ANY)] * 5,
        out_specs=[pl.BlockSpec(memory_space=pltpu.VMEM)] * 3,
        scratch_shapes=(
            buffers((far, 2)) + buffers((far, 2)) + buffers((far,)) + buffers((far,))
            + buffers((far - 1,))
            + [pltpu.VMEM(x.shape, x.dtype) for x in loads]
            + [pltpu.VMEM(s, half) for s in shapes]
            + [
                pltpu.VMEM((rows, own_hid), single),
                pltpu.VMEM((rows, own_hid), half),
                pltpu.VMEM((own_hid, rows), half),
                swapped,
                swapped,
                pltpu.VMEM((rows, hid), single),
                pltpu.VMEM((rows, hid), half),
                pltpu.VMEM((hid, rows), half),
                pltpu.VMEM((rows, own_width), half),
                swapped,
                swapped,
                pltpu.VMEM((rows, hid), half),
                pltpu.VMEM((hid, rows), half),
                pltpu.SemaphoreType.DMA((5,)),
                pltpu.SemaphoreType.DMA((2, blocks)),
                pltpu.SemaphoreType.DMA((2, blocks)),
                pltpu.VMEM((8, LANES), jnp.float32),
                pltpu.VMEM((n_dp * n_mp - 1, 8, LANES), jnp.float32),
                pltpu.SemaphoreType.DMA((2, flat)),
                pltpu.SemaphoreType.DMA((2, flat)),
                pltpu.SemaphoreType.DMA((flat, far - 1)),
                pltpu.SemaphoreType.DMA((flat, far - 1)),
                pltpu.SemaphoreType.DMA((2,)),
            ]
        ),
        compiler_params=pltpu.CompilerParams(
            collective_id=0, has_side_effects=True, vmem_limit_bytes=60 * 1024 * 1024
        ),
    )(counts, *loads)
    return first[:, :in_width].T, middle.T, last[:, :own_width]


def solution(mesh):
    return jax.shard_map(
        functools.partial(per_device, (mesh.shape["dp"], mesh.shape["mp"])),
        mesh=mesh,
        in_specs=(
            P("dp", None),
            P("dp", None),
            P("dp"),
            P(None, "mp"),
            P("mp", None),
            P(None, "mp"),
        ),
        out_specs=(P(None, ("mp", "dp")), P("mp", "dp"), P("dp", "mp")),
        check_vma=False,
    )
```

profile of v0, /device:TPU:0, one launch (start us, length us, event | category | flops | bytes accessed | tf_op | source)
XLA Modules:
  0.0 124.6 jit_solution(16042250961913007140)
XLA Ops:
  0.6 0.0 copy-start
  0.6 2.4 %copy.10.refs_2_ = bf16[256,1326]{1,0:T(8,128)(2,1)} copy(bf16[256,1326]{0,1:T(8,128)(2,1)} %param.7) | data formatting | bytes 1357824 | tf_op args[1]
  3.0 2.5 %copy.9.refs_1_ = bf16[256,2652]{1,0:T(8,128)(2,1)} copy(bf16[256,2652]{0,1:T(8,128)(2,1)} %param.6) | data formatting | bytes 2715648 | tf_op args[0]
  5.5 0.0 copy-done
  5.5 2.4 %copy.11.refs_5_ = bf16[1536,663]{1,0:T(8,128)(2,1)} copy(bf16[1536,663]{0,1:T(8,128)(2,1)S(1)} %copy-done) | data formatting | bytes 4073472 | tf_op args[5]
  8.0 111.4 %shard_map.85 = (f32[48,2688]{1,0:T(8,128)}, f32[96,768]{1,0:T(8,128)}, f32[96,768]{1,0:T(8,128)}) custom-call(s32[2]{0:T(128)} %refs_0_.1, bf16[256,2652]{1,0:T(8,128)(2,1)} %copy.9.refs_1_, bf16[256,1326]{1,0:T(8,128)(2,1)} %copy.10.refs_2_, bf16[2652,768]{1,0:T(8,128)(2,1)} %refs_3_.1, bf16[768,1536]{1,0:T(8,128)(2,1)} %refs_4_.1, ...), custom_call_target="tpu_custom_call" | custom-call | tf_op jit(solution)/shard_map/pallas_call | solution.py:334
  119.3 1.9 %slice_bitcast_fusion = f32[2652,48]{0,1:T(8,128)} fusion(f32[48,2688]{1,0:T(8,128)} %get-tuple-element.6), kind=kLoop, calls=%fused_computation | loop fusion | bytes 1018368 | tf_op jit(solution)/shard_map/transpose | solution.py:375
  121.2 1.7 %copy.14 = f32[768,96]{0,1:T(8,128)} copy(f32[768,96]{0,1:T(8,128)} %bitcast.5) | data formatting | bytes 589824
  122.9 1.7 %copy.15 = f32[96,663]{1,0:T(8,128)} copy(f32[96,663]{1,0:T(8,128)} %bitcast.4) | data formatting | bytes 509184
Async XLA Ops:
  0.6 4.9 %copy-start = (bf16[1536,663]{0,1:T(8,128)(2,1)S(1)}, bf16[1536,663]{0,1:T(8,128)(2,1)}, u32[]{:S(2)}) copy-start(bf16[1536,663]{0,1:T(8,128)(2,1)} %param.11) | copy-start | bytes 6110212
where the time goes:
time: 125 us
  Pallas kernels  111 us (89%)
  local copies, waits for them, and re-layouts  12.6 us (10%)
    pallas_call x1, Pallas kernels, per_device(): pl.pallas_call(functools.partial(step_kernel, dims, params, pairs, blocks...  111 us
    unnamed x7, local copies, waits for them, and re-layouts  10.7 us

commit v1 on v0

v1 whole, which is shorter than its diff:
```python
import functools
import math

import jax
import jax.numpy as jnp
from jax import lax
from jax.experimental import pallas as pl
from jax.experimental.pallas import tpu as pltpu
from jax.sharding import PartitionSpec as P

BLOCK = 128
LANES = 128
MESH = pl.DeviceIdType.MESH
FIRST, MIDDLE, LAST = 0, 1, 2
NT = (((1,), (1,)), ((), ()))


def silu_slope(pre_act):
    sigmoid_of = jax.nn.sigmoid(pre_act)
    return sigmoid_of * (1.0 + pre_act * (1.0 - sigmoid_of))


def pad_to(size, step):
    return -(-size // step) * step


def orders_of(n_dp):
    bits = n_dp.bit_length() - 1
    heads = {FIRST: (0, 1), MIDDLE: (2, 0, 1), LAST: (1, 0)}
    return {
        which: head + tuple(b for b in range(bits) if b not in head)
        for which, head in heads.items()
    }


def pieces_of(wide):
    out = []
    for which, keys in (
        (MIDDLE, (27, 33)),
        (FIRST, (28, 34, 41, 47)),
        (LAST, (39, 45)),
    ):
        tiles = wide[which] // LANES
        parts = len(keys)
        bounds = [round(tiles * i / parts) * LANES for i in range(parts + 1)]
        for i, key in enumerate(keys):
            out.append((which, bounds[i], bounds[i + 1] - bounds[i], key))
    return out


def step_kernel(dims, params, orders, pieces, stage_shapes, *refs):
    n_dp, n_mp = dims
    stages = n_dp.bit_length() - 2
    count = len(pieces)
    counts, loads, outs, scale_out = refs[0], refs[1:6], refs[6:9], refs[9]
    refs = refs[10:]
    held = [refs[k * count : (k + 1) * count] for k in range(stages)]
    refs = refs[stages * count :]
    got = [refs[k * count : (k + 1) * count] for k in range(stages)]
    refs = refs[stages * count :]
    belief_t, target_t, w_first, w_middle, w_last_t = refs[:5]
    parts_t, near_t = refs[5:8], refs[8:11]
    (
        belief, near_belief, pre1, act1, near_act1, part2, other2, pre2, act2, slope_out, near_out,
        part_back, other_back, slope2, slope1, load_sems, swap_send, swap_got, share_send, share_got,
        sends, gots, sq_send, sq_got, sq_sems,
    ) = refs[11:]

    in_width, own_hid = w_first.shape
    own_width, hid = w_last_t.shape
    rows = belief.shape[0]
    blocks = part2.shape[0]
    block = hid // blocks

    landing = (belief_t, target_t, w_first, w_middle, w_last_t)
    arrivals = [
        pltpu.make_async_copy(src, dst, load_sems.at[i])
        for i, (src, dst) in enumerate(zip(loads, landing))
    ]
    for i in (0, 2, 3, 4, 1):
        arrivals[i].start()

    dp, mp = lax.axis_index("dp"), lax.axis_index("mp")
    me = dp * n_mp + mp
    total = n_dp * n_mp

    def side(bit):
        return (dp // (1 << bit)) % 2

    def peer(bit):
        return (dp + (1 - 2 * side(bit)) * (1 << bit), mp)

    sibling = (dp, 1 - mp)
    barrier = pltpu.get_barrier_semaphore()

    def greet(j, _):
        other = lax.rem(me + j, total)
        pl.semaphore_signal(
            barrier, inc=1, device_id=(other // n_mp, other % n_mp), device_id_type=MESH
        )
        return 0

    lax.fori_loop(1, total, greet, 0)

    def remote(src, dst, sems, k, goal):
        return pltpu.make_async_remote_copy(
            src, dst, sems[0].at[k], sems[1].at[k], device_id=goal, device_id_type=MESH
        )

    share = functools.partial(remote, sems=(share_send, share_got))
    my_rows = pl.ds(pl.multiple_of(mp * (rows // 2), rows // 2), rows // 2)
    pair = {which: orders[which][0] for which in orders}
    away = {which: 1 - side(pair[which]) for which in orders}
    home = {which: side(pair[which]) for which in orders}
    send_belief = share(
        belief.at[my_rows, :], near_belief.at[my_rows, :], k=0, goal=peer(pair[FIRST])
    )
    send_act1 = share(act1, near_act1, k=1, goal=peer(pair[MIDDLE]))
    send_act2 = share(
        parts_t[LAST].at[away[LAST], mp], near_t[LAST].at[mp], k=2, goal=peer(pair[LAST])
    )
    send_out = share(slope_out, near_out, k=3, goal=peer(pair[LAST]))
    send_slope2 = share(
        parts_t[MIDDLE].at[away[MIDDLE], mp], near_t[MIDDLE].at[mp], k=4, goal=peer(pair[MIDDLE])
    )
    send_slope1 = share(parts_t[FIRST].at[away[FIRST]], near_t[FIRST], k=5, goal=peer(pair[FIRST]))
    pass_belief = share(
        near_belief.at[my_rows, :], near_belief.at[my_rows, :], k=6, goal=sibling
    )
    pass_act2 = share(near_t[LAST].at[mp], near_t[LAST].at[mp], k=7, goal=sibling)
    pass_slope2 = share(near_t[MIDDLE].at[mp], near_t[MIDDLE].at[mp], k=8, goal=sibling)

    def swap(way, part, other, i):
        return pltpu.make_async_remote_copy(
            part.at[i], other.at[i], swap_send.at[way, i], swap_got.at[way, i],
            device_id=sibling, device_id_type=MESH,
        )

    def transpose_parts(which, source, width):
        order = orders[which]
        r = width // n_dp
        step = math.lcm(r, LANES)
        for start in range(0, width, step):
            value = source[:, start : start + step].T
            for d in range(start // r, (start + step) // r):
                where = [(d >> bit) & 1 for bit in order]
                at = 0
                for bit in where[2:]:
                    at = 2 * at + bit
                parts_t[which][where[0], where[1], at * r : (at + 1) * r, :] = value[
                    d * r - start : (d + 1) * r - start
                ]

    rights = {FIRST: (belief, near_belief), MIDDLE: (act1, near_act1), LAST: (slope_out, near_out)}

    def weight_grad(p, half):
        which, start, width, _ = pieces[p]
        own, near = rights[which]
        value = jnp.dot(
            parts_t[which][home[which], half], own[:, start : start + width],
            preferred_element_type=jnp.float32,
        ) + jnp.dot(
            near_t[which][half], near[:, start : start + width],
            preferred_element_type=jnp.float32,
        )
        store(p, 0, half, value)

    def store(p, k, half, value):
        ref = held[k][p]
        if k == stages - 1:
            ref[half] = value.astype(jnp.bfloat16)
            return
        h = value.shape[0] // 2
        ref[half, 0] = value[:h].astype(jnp.bfloat16)
        ref[half, 1] = value[h:].astype(jnp.bfloat16)

    def exchange(p, k):
        bit = orders[pieces[p][0]][1 + k]
        return pltpu.make_async_remote_copy(
            held[k][p].at[1 - side(bit)], got[k][p], sends.at[k, p], gots.at[k, p],
            device_id=peer(bit), device_id_type=MESH,
        )

    def send_grad(p):
        weight_grad(p, 1 - side(orders[pieces[p][0]][1]))
        exchange(p, 0).start()

    def keep_grad(p):
        weight_grad(p, side(orders[pieces[p][0]][1]))

    arrivals[0].wait()
    for start in range(0, belief.shape[1], LANES * 3):
        value = belief_t[start : min(start + LANES * 3, in_width), :]
        if value.shape[0] < LANES * 3:
            value = jnp.concatenate(
                [value, jnp.zeros((LANES * 3 - value.shape[0], rows), jnp.bfloat16)], axis=0
            )
        belief[:, start : start + LANES * 3] = value.T
    pl.semaphore_wait(barrier, total - 1)
    send_belief.start()
    arrivals[2].wait()
    for c in range(0, own_hid, 256):
        value = jnp.dot(
            belief[:, :in_width], w_first[:, c : c + 256], preferred_element_type=jnp.float32
        )
        pre1[:, c : c + 256] = value
        act1[:, c : c + 256] = jax.nn.silu(value).astype(jnp.bfloat16)
    send_act1.start()
    arrivals[3].wait()
    for i in range(blocks):
        part2[i] = jnp.dot(
            act1[...], w_middle[:, i * block : (i + 1) * block],
            preferred_element_type=jnp.float32,
        )
        swap(0, part2, other2, i).start()
    arrivals[1].wait()
    arrivals[4].wait()
    row = lax.broadcasted_iota(jnp.int32, (rows, 1), 0)
    limit = jnp.full((rows, 1), counts[0], jnp.int32)
    for b in range(1, rows // BLOCK):
        limit = jnp.where(row >= b * BLOCK, counts[b] + b * BLOCK, limit)
    live = jnp.where(row < limit, 1.0, 0.0)
    target = target_t[...].T
    wanted = target[:, :own_width].astype(jnp.float32)
    for m in range(1, n_mp):
        wanted = jnp.where(
            mp == m, target[:, m * own_width : (m + 1) * own_width].astype(jnp.float32), wanted
        )
    for i in range(blocks):
        cols = slice(i * block, (i + 1) * block)
        swap(0, part2, other2, i).wait_recv()
        value = part2[i] + other2[i]
        pre2[:, cols] = value
        act2[:, cols] = jax.nn.silu(value).astype(jnp.bfloat16)
    transpose_parts(LAST, act2, hid)
    send_act2.start()
    predicted = lax.dot_general(act2[...], w_last_t[...], NT, preferred_element_type=jnp.float32)
    value = jnp.clip(predicted - wanted, -1.0, 1.0) * live
    slope_out[...] = jnp.concatenate(
        [value, jnp.zeros((rows, slope_out.shape[1] - own_width), jnp.float32)], axis=1
    ).astype(jnp.bfloat16)
    send_out.start()

    for i in range(blocks):
        part_back[i] = jnp.dot(
            slope_out[:, :own_width], w_last_t[:, i * block : (i + 1) * block],
            preferred_element_type=jnp.float32,
        )
        swap(1, part_back, other_back, i).start()
    for i in range(blocks):
        cols = slice(i * block, (i + 1) * block)
        swap(1, part_back, other_back, i).wait_recv()
        value = (part_back[i] + other_back[i]) * silu_slope(pre2[:, cols])
        slope2[:, cols] = value.astype(jnp.bfloat16)
    transpose_parts(MIDDLE, slope2, hid)
    send_slope2.start()
    for c in range(0, own_hid, 256):
        back = lax.dot_general(
            slope2[...], w_middle[c : c + 256, :], NT, preferred_element_type=jnp.float32
        )
        slope1[:, c : c + 256] = (back * silu_slope(pre1[:, c : c + 256])).astype(jnp.bfloat16)
    transpose_parts(FIRST, slope1, own_hid)
    send_slope1.start()

    send_act2.wait_recv()
    pass_act2.start()
    send_belief.wait_recv()
    pass_belief.start()
    send_slope2.wait_recv()
    pass_slope2.start()
    send_act1.wait_recv()
    pass_slope2.wait_recv()
    by_layer = {which: [p for p in range(count) if pieces[p][0] == which] for which in orders}
    late = by_layer[FIRST][2:]
    for p in by_layer[MIDDLE]:
        send_grad(p)
    pass_belief.wait_recv()
    send_slope1.wait_recv()
    for p in by_layer[FIRST][:2]:
        send_grad(p)
    pass_act2.wait_recv()
    send_out.wait_recv()
    for p in by_layer[LAST]:
        send_grad(p)
    for p in range(count):
        if p not in late:
            keep_grad(p)

    steps = sorted(
        (pieces[p][3] + 7 * k, k, p) for p in range(count) for k in range(stages - 1)
    )
    for _, k, p in steps:
        if late:
            send_grad(late[0])
            keep_grad(late[0])
            late = late[1:]
        bit = orders[pieces[p][0]][1 + k]
        exchange(p, k).wait_recv()
        for h in range(2):
            value = held[k][p][side(bit), h].astype(jnp.float32) + got[k][p][h].astype(jnp.float32)
            store(p, k + 1, h, value)
        exchange(p, k + 1).start()

    squares = jnp.float32(0.0)
    for p in sorted(range(count), key=lambda p: pieces[p][3]):
        which, start, width, _ = pieces[p]
        k = stages - 1
        bit = orders[which][1 + k]
        exchange(p, k).wait_recv()
        value = held[k][p][side(bit)].astype(jnp.float32) + got[k][p][...].astype(jnp.float32)
        outs[which][:, start : start + width] = value
        squares = squares + jnp.sum(value * value)

    sq_send[...] = jnp.full(sq_send.shape, squares, jnp.float32)

    def square_copy(j):
        other = lax.rem(me + j, total)
        return pltpu.make_async_remote_copy(
            sq_send, sq_got.at[j - 1], sq_sems.at[0], sq_sems.at[1],
            device_id=(other // n_mp, other % n_mp), device_id_type=MESH,
        )

    def tell(j, _):
        square_copy(j).start()
        return 0

    lax.fori_loop(1, total, tell, 0)
    for i in range(blocks):
        swap(0, part2, other2, i).wait_send()
        swap(1, part_back, other_back, i).wait_send()
    for copy in (
        send_belief, send_act1, send_act2, send_out, send_slope2, send_slope1,
        pass_belief, pass_act2, pass_slope2,
    ):
        copy.wait_send()
    for p in range(count):
        for k in range(stages):
            exchange(p, k).wait_send()
    pltpu.make_async_copy(sq_got, sq_got, sq_sems.at[1]).wait()
    everyone = squares + jnp.sum(sq_got[...]) * (1.0 / (sq_send.shape[0] * sq_send.shape[1]))
    scale_out[...] = lax.rsqrt(
        jnp.full(scale_out.shape, everyone / params + 1e-06, jnp.float32)
    )
    pltpu.make_async_copy(sq_got, sq_got, sq_sems.at[0]).wait()


def scale_kernel(scale, *refs):
    factor = scale[0:1, 0:1]
    for raw, out in zip(refs[:3], refs[3:]):
        out[...] = raw[:, : out.shape[1]] * factor


def per_device(dims, belief, target_value, counts, w_first, w_middle, w_last):
    n_dp, n_mp = dims
    stages = n_dp.bit_length() - 2
    blocks = 3
    rows, (in_width, own_hid) = belief.shape[0], w_first.shape
    hid, own_width = w_last.shape
    params = float(n_mp * (w_first.size + w_middle.size + w_last.size))
    long = {FIRST: own_hid, MIDDLE: hid, LAST: hid}
    wide = {
        FIRST: pad_to(in_width, LANES),
        MIDDLE: pad_to(own_hid, LANES),
        LAST: pad_to(own_width, LANES),
    }
    layers = (FIRST, MIDDLE, LAST)
    orders = orders_of(n_dp)
    pieces = pieces_of(wide)
    half, single = jnp.bfloat16, jnp.float32

    def stage_shape(piece, k):
        r = long[piece[0]] // 2 >> (k + 1)
        return (2, r, piece[2]) if k == stages - 1 else (2, 2, r // 2, piece[2])

    shapes = [[stage_shape(piece, k) for piece in pieces] for k in range(stages)]
    loads = (belief.T, target_value.T, w_first, w_middle, w_last.T)
    swapped = pltpu.VMEM((blocks, rows, hid // blocks), single)
    count = len(pieces)
    raws = pl.pallas_call(
        functools.partial(step_kernel, dims, params, orders, pieces, shapes),
        out_shape=[
            jax.ShapeDtypeStruct((long[w] // n_dp, wide[w]), single) for w in layers
        ] + [jax.ShapeDtypeStruct((8, LANES), single)],
        in_specs=[pl.BlockSpec(memory_space=pltpu.SMEM)]
        + [pl.BlockSpec(memory_space=pl.ANY)] * 5,
        out_specs=[pl.BlockSpec(memory_space=pltpu.VMEM)] * 4,
        scratch_shapes=(
            [pltpu.VMEM(s, half) for stage in shapes for s in stage]
            + [pltpu.VMEM(s[1:], half) for stage in shapes for s in stage]
            + [
                pltpu.VMEM((in_width, rows), half),
                pltpu.VMEM((n_mp * own_width, rows), half),
                pltpu.VMEM(w_first.shape, half),
                pltpu.VMEM(w_middle.shape, half),
                pltpu.VMEM((own_width, hid), half),
            ]
            + [pltpu.VMEM((2, 2, long[w] // 4, rows), half) for w in layers]
            + [pltpu.VMEM((2, long[w] // 4, rows), half) for w in layers]
            + [
                pltpu.VMEM((rows, wide[FIRST]), half),
                pltpu.VMEM((rows, wide[FIRST]), half),
                pltpu.VMEM((rows, own_hid), single),
                pltpu.VMEM((rows, own_hid), half),
                pltpu.VMEM((rows, own_hid), half),
                swapped,
                swapped,
                pltpu.VMEM((rows, hid), single),
                pltpu.VMEM((rows, hid), half),
                pltpu.VMEM((rows, wide[LAST]), half),
                pltpu.VMEM((rows, wide[LAST]), half),
                swapped,
                swapped,
                pltpu.VMEM((rows, hid), half),
                pltpu.VMEM((rows, own_hid), half),
                pltpu.SemaphoreType.DMA((5,)),
                pltpu.SemaphoreType.DMA((2, blocks)),
                pltpu.SemaphoreType.DMA((2, blocks)),
                pltpu.SemaphoreType.DMA((9,)),
                pltpu.SemaphoreType.DMA((9,)),
                pltpu.SemaphoreType.DMA((stages, count)),
                pltpu.SemaphoreType.DMA((stages, count)),
                pltpu.VMEM((8, LANES), single),
                pltpu.VMEM((n_dp * n_mp - 1, 8, LANES), single),
                pltpu.SemaphoreType.DMA((2,)),
            ]
        ),
        compiler_params=pltpu.CompilerParams(
            collective_id=0, has_side_effects=True, vmem_limit_bytes=60 * 1024 * 1024
        ),
    )(counts, *loads)
    finals = (
        (long[FIRST] // n_dp, in_width),
        (long[MIDDLE] // n_dp, own_hid),
        (long[LAST] // n_dp, own_width),
    )
    first, middle, last = pl.pallas_call(
        scale_kernel,
        out_shape=[jax.ShapeDtypeStruct(s, single) for s in finals],
        in_specs=[pl.BlockSpec(memory_space=pltpu.VMEM)] * 4,
        out_specs=[pl.BlockSpec(memory_space=pltpu.VMEM)] * 3,
    )(raws[3], *raws[:3])
    return first.T, middle.T, last


def solution(mesh):
    return jax.shard_map(
        functools.partial(per_device, (mesh.shape["dp"], mesh.shape["mp"])),
        mesh=mesh,
        in_specs=(
            P("dp", None),
            P("dp", None),
            P("dp"),
            P(None, "mp"),
            P("mp", None),
            P(None, "mp"),
        ),
        out_specs=(P(None, ("mp", "dp")), P("mp", "dp"), P("dp", "mp")),
        check_vma=False,
    )
```

time: 125 us -> 90.7 us (0.73)
  Pallas kernels: 111 us -> 89.9 us
  local copies, waits for them, and re-layouts: 12.6 us -> 0 us
    pallas_call x1 -> x2, Pallas kernels: 111 us -> 89.9 us  [the longest x1 87.6 us: per_device(): pl.pallas_call(functools.partial(step_kernel, dims, params, orders, piece...]
    unnamed x7 -> x0, local copies, waits for them, and re-layouts: 10.7 us -> none
    transpose x1 -> x0, local copies, waits for them, and re-layouts: 1.86 us -> none  [per_device(): return (first[:, :in_width].T, middle.T, last[:, :own_width])]
where the time goes in v1:
time: 90.7 us; the launch traced here: 90.5 us
  Pallas kernels  89.9 us (99%)
    pallas_call x1, Pallas kernels, per_device(): pl.pallas_call(functools.partial(step_kernel, dims, params, orders, piece...  87.6 us
    pallas_call x1, Pallas kernels, per_device(): pl.pallas_call(scale_kernel, out_shape=[jax.ShapeDtypeStruct(s, single) f...  2.25 us

profile of v1, /device:TPU:0, one launch (start us, length us, event | category | flops | bytes accessed | tf_op | source)
XLA Modules:
  0.0 90.5 jit_solution(13838127406251638650)
XLA Ops:
  0.6 87.6 %shard_map.85 = (f32[48,2688]{1,0:T(8,128)}, f32[96,768]{1,0:T(8,128)}, f32[96,768]{1,0:T(8,128)}, f32[8,128]{1,0:T(8,128)}) custom-call(s32[2]{0:T(128)} %refs_0_.1, bf16[2652,256]{1,0:T(8,128)(2,1)} %bitcast.6, bf16[1326,256]{1,0:T(8,128)(2,1)} %bitcast.7, bf16[2652,768]{1,0:T(8,128)(2,1)} %refs_3_.1, bf16[768,1536]{1,0:T(8,128)(2,1)} %refs_4_.1, ...), custom_call_target="tpu_custom_call" | custom-call | tf_op jit(solution)/shard_map/pallas_call | solution.py:379
  88.3 2.2 %shard_map.86 = (f32[48,2652]{1,0:T(8,128)}, f32[96,768]{1,0:T(8,128)}, f32[96,663]{1,0:T(8,128)}) custom-call(f32[8,128]{1,0:T(8,128)} %get-tuple-element.10.scale, f32[48,2688]{1,0:T(8,128)} %get-tuple-element.11.refs_0_, f32[96,768]{1,0:T(8,128)} %get-tuple-element.12.refs_1_, f32[96,768]{1,0:T(8,128)} %get-tuple-element.13.refs_2_), custom_call_target="tpu_custom_call" | custom-call | tf_op jit(solution)/shard_map/pallas_call | solution.py:436

commit v2 on v1

--- a/solution.py
+++ b/solution.py
@@ -26,38 +26,38 @@
 
 def orders_of(n_dp):
     bits = n_dp.bit_length() - 1
-    heads = {FIRST: (0, 1), MIDDLE: (2, 0, 1), LAST: (1, 0)}
+    heads = {FIRST: ((0, 1), (2,)), MIDDLE: ((2,), (1, 0)), LAST: ((2,), (0, 1))}
     return {
-        which: head + tuple(b for b in range(bits) if b not in head)
-        for which, head in heads.items()
+        which: (shared, head + tuple(b for b in range(bits) if b not in shared + head))
+        for which, (shared, head) in heads.items()
     }
 
 
 def pieces_of(wide):
     out = []
-    for which, keys in (
-        (MIDDLE, (27, 33)),
-        (FIRST, (28, 34, 41, 47)),
-        (LAST, (39, 45)),
+    for which, table in (
+        (LAST, ((36.7, 44.6, 50), (43, 51, 55))),
+        (FIRST, ((36, 41), (38.7, 44), (41.8, 47), (44.5, 49))),
+        (MIDDLE, ((41.5, 46.8, 52), (47.8, 53, 57))),
     ):
         tiles = wide[which] // LANES
-        parts = len(keys)
+        parts = len(table)
         bounds = [round(tiles * i / parts) * LANES for i in range(parts + 1)]
-        for i, key in enumerate(keys):
-            out.append((which, bounds[i], bounds[i + 1] - bounds[i], key))
+        for i, keys in enumerate(table):
+            out.append((which, bounds[i], bounds[i + 1] - bounds[i], keys))
     return out
 
 
 def step_kernel(dims, params, orders, pieces, stage_shapes, *refs):
     n_dp, n_mp = dims
-    stages = n_dp.bit_length() - 2
     count = len(pieces)
     counts, loads, outs, scale_out = refs[0], refs[1:6], refs[6:9], refs[9]
     refs = refs[10:]
-    held = [refs[k * count : (k + 1) * count] for k in range(stages)]
-    refs = refs[stages * count :]
-    got = [refs[k * count : (k + 1) * count] for k in range(stages)]
-    refs = refs[stages * count :]
+    held, got = [], []
+    for group in (held, got):
+        for shapes in stage_shapes:
+            group.append(refs[: len(shapes)])
+            refs = refs[len(shapes) :]
     belief_t, target_t, w_first, w_middle, w_last_t = refs[:5]
     parts_t, near_t = refs[5:8], refs[8:11]
     (
@@ -109,26 +109,33 @@
 
     share = functools.partial(remote, sems=(share_send, share_got))
     my_rows = pl.ds(pl.multiple_of(mp * (rows // 2), rows // 2), rows // 2)
-    pair = {which: orders[which][0] for which in orders}
-    away = {which: 1 - side(pair[which]) for which in orders}
-    home = {which: side(pair[which]) for which in orders}
-    send_belief = share(
-        belief.at[my_rows, :], near_belief.at[my_rows, :], k=0, goal=peer(pair[FIRST])
+    x, y = (side(bit) for bit in orders[FIRST][0])
+    x_peer, y_peer = (peer(bit) for bit in orders[FIRST][0])
+    diagonal = (x_peer[0] + y_peer[0] - dp, mp)
+    (low,) = orders[MIDDLE][0]
+    z, z_peer = side(low), peer(low)
+    belief_x = share(belief.at[my_rows, :], near_belief.at[0, my_rows, :], k=0, goal=x_peer)
+    belief_y = share(belief.at[my_rows, :], near_belief.at[1, my_rows, :], k=1, goal=y_peer)
+    relay_goal = (jnp.where(mp == 0, y_peer[0], x_peer[0]), mp)
+    relay = share(
+        near_belief.at[mp, my_rows, :], near_belief.at[2, my_rows, :], k=2, goal=relay_goal
     )
-    send_act1 = share(act1, near_act1, k=1, goal=peer(pair[MIDDLE]))
-    send_act2 = share(
-        parts_t[LAST].at[away[LAST], mp], near_t[LAST].at[mp], k=2, goal=peer(pair[LAST])
-    )
-    send_out = share(slope_out, near_out, k=3, goal=peer(pair[LAST]))
-    send_slope2 = share(
-        parts_t[MIDDLE].at[away[MIDDLE], mp], near_t[MIDDLE].at[mp], k=4, goal=peer(pair[MIDDLE])
-    )
-    send_slope1 = share(parts_t[FIRST].at[away[FIRST]], near_t[FIRST], k=5, goal=peer(pair[FIRST]))
-    pass_belief = share(
-        near_belief.at[my_rows, :], near_belief.at[my_rows, :], k=6, goal=sibling
-    )
-    pass_act2 = share(near_t[LAST].at[mp], near_t[LAST].at[mp], k=7, goal=sibling)
-    pass_slope2 = share(near_t[MIDDLE].at[mp], near_t[MIDDLE].at[mp], k=8, goal=sibling)
+    passes = [
+        share(near_belief.at[i, my_rows, :], near_belief.at[i, my_rows, :], k=3 + i, goal=sibling)
+        for i in range(3)
+    ]
+    slopes = [
+        share(parts_t[FIRST].at[at], near_t[FIRST].at[i], k=6 + i, goal=goal)
+        for i, (at, goal) in enumerate(
+            (((1 - x, y), x_peer), ((x, 1 - y), y_peer), ((1 - x, 1 - y), diagonal))
+        )
+    ]
+    send_act1 = share(act1, near_act1, k=9, goal=z_peer)
+    send_act2 = share(parts_t[LAST].at[1 - z, mp], near_t[LAST].at[mp], k=10, goal=z_peer)
+    send_out = share(slope_out, near_out, k=11, goal=z_peer)
+    send_slope2 = share(parts_t[MIDDLE].at[1 - z, mp], near_t[MIDDLE].at[mp], k=12, goal=z_peer)
+    pass_act2 = share(near_t[LAST].at[mp], near_t[LAST].at[mp], k=13, goal=sibling)
+    pass_slope2 = share(near_t[MIDDLE].at[mp], near_t[MIDDLE].at[mp], k=14, goal=sibling)
 
     def swap(way, part, other, i):
         return pltpu.make_async_remote_copy(
@@ -137,7 +144,7 @@
         )
 
     def transpose_parts(which, source, width):
-        order = orders[which]
+        order = orders[which][0] + orders[which][1]
         r = width // n_dp
         step = math.lcm(r, LANES)
         for start in range(0, width, step):
@@ -151,23 +158,35 @@
                     d * r - start : (d + 1) * r - start
                 ]
 
-    rights = {FIRST: (belief, near_belief), MIDDLE: (act1, near_act1), LAST: (slope_out, near_out)}
-
-    def weight_grad(p, half):
+    def dot(left, right):
+        return jnp.dot(left, right, preferred_element_type=jnp.float32)
+
+    def first_grad(p):
+        _, start, width, _ = pieces[p]
+        cols = slice(start, start + width)
+        value = dot(parts_t[FIRST][x, y], belief[:, cols])
+        for i in range(3):
+            value = value + dot(near_t[FIRST][i], near_belief[i, :, cols])
+        h = value.shape[0] // 2
+        store(p, 0, 0, value[:h])
+        store(p, 0, 1, value[h:])
+        exchange(p, 0).start()
+
+    rights = {MIDDLE: (act1, near_act1), LAST: (slope_out, near_out)}
+
+    def pair_grad(p, half):
         which, start, width, _ = pieces[p]
         own, near = rights[which]
-        value = jnp.dot(
-            parts_t[which][home[which], half], own[:, start : start + width],
-            preferred_element_type=jnp.float32,
-        ) + jnp.dot(
-            near_t[which][half], near[:, start : start + width],
-            preferred_element_type=jnp.float32,
-        )
+        cols = slice(start, start + width)
+        value = dot(parts_t[which][z, half], own[:, cols]) + dot(near_t[which][half], near[:, cols])
         store(p, 0, half, value)
 
+    def stages_of(p):
+        return len(orders[pieces[p][0]][1])
+
     def store(p, k, half, value):
-        ref = held[k][p]
-        if k == stages - 1:
+        ref = held[p][k]
+        if k == stages_of(p) - 1:
             ref[half] = value.astype(jnp.bfloat16)
             return
         h = value.shape[0] // 2
@@ -175,18 +194,18 @@
         ref[half, 1] = value[h:].astype(jnp.bfloat16)
 
     def exchange(p, k):
-        bit = orders[pieces[p][0]][1 + k]
+        bit = orders[pieces[p][0]][1][k]
         return pltpu.make_async_remote_copy(
-            held[k][p].at[1 - side(bit)], got[k][p], sends.at[k, p], gots.at[k, p],
+            held[p][k].at[1 - side(bit)], got[p][k], sends.at[p, k], gots.at[p, k],
             device_id=peer(bit), device_id_type=MESH,
         )
 
     def send_grad(p):
-        weight_grad(p, 1 - side(orders[pieces[p][0]][1]))
+        pair_grad(p, 1 - side(orders[pieces[p][0]][1][0]))
         exchange(p, 0).start()
 
     def keep_grad(p):
-        weight_grad(p, side(orders[pieces[p][0]][1]))
+        pair_grad(p, side(orders[pieces[p][0]][1][0]))
 
     arrivals[0].wait()
     for start in range(0, belief.shape[1], LANES * 3):
@@ -197,7 +216,8 @@
             )
         belief[:, start : start + LANES * 3] = value.T
     pl.semaphore_wait(barrier, total - 1)
-    send_belief.start()
+    belief_x.start()
+    belief_y.start()
     arrivals[2].wait()
     for c in range(0, own_hid, 256):
         value = jnp.dot(
@@ -260,56 +280,63 @@
         )
         slope1[:, c : c + 256] = (back * silu_slope(pre1[:, c : c + 256])).astype(jnp.bfloat16)
     transpose_parts(FIRST, slope1, own_hid)
-    send_slope1.start()
-
+    for copy in slopes:
+        copy.start()
+
+    by_layer = {which: [p for p in range(count) if pieces[p][0] == which] for which in orders}
     send_act2.wait_recv()
     pass_act2.start()
-    send_belief.wait_recv()
-    pass_belief.start()
-    send_slope2.wait_recv()
-    pass_slope2.start()
-    send_act1.wait_recv()
-    pass_slope2.wait_recv()
-    by_layer = {which: [p for p in range(count) if pieces[p][0] == which] for which in orders}
-    late = by_layer[FIRST][2:]
-    for p in by_layer[MIDDLE]:
-        send_grad(p)
-    pass_belief.wait_recv()
-    send_slope1.wait_recv()
-    for p in by_layer[FIRST][:2]:
-        send_grad(p)
+    belief_x.wait_recv()
+    belief_y.wait_recv()
+    relay.start()
+    passes[0].start()
+    passes[1].start()
     pass_act2.wait_recv()
     send_out.wait_recv()
     for p in by_layer[LAST]:
         send_grad(p)
+    for p in by_layer[LAST]:
+        keep_grad(p)
+    relay.wait_recv()
+    passes[2].start()
+    send_slope2.wait_recv()
+    pass_slope2.start()
+    slopes[0].wait_recv()
+    slopes[1].wait_recv()
+    slopes[2].wait_recv()
+    passes[0].wait_recv()
+    passes[1].wait_recv()
+    passes[2].wait_recv()
+    for p in by_layer[FIRST][:2]:
+        first_grad(p)
+    send_act1.wait_recv()
+    pass_slope2.wait_recv()
+    for p in by_layer[MIDDLE]:
+        send_grad(p)
+    for p in by_layer[FIRST][2:]:
+        first_grad(p)
+    for p in by_layer[MIDDLE]:
+        keep_grad(p)
+
+    steps = []
     for p in range(count):
-        if p not in late:
-            keep_grad(p)
-
-    steps = sorted(
-        (pieces[p][3] + 7 * k, k, p) for p in range(count) for k in range(stages - 1)
-    )
-    for _, k, p in steps:
-        if late:
-            send_grad(late[0])
-            keep_grad(late[0])
-            late = late[1:]
-        bit = orders[pieces[p][0]][1 + k]
+        keys = pieces[p][3]
+        for k in range(stages_of(p)):
+            steps.append((keys[min(k, len(keys) - 1)] + 7 * max(0, k + 1 - len(keys)), k, p))
+    squares = jnp.float32(0.0)
+    for _, k, p in sorted(steps):
+        which, start, width, _ = pieces[p]
+        mine = side(orders[which][1][k])
         exchange(p, k).wait_recv()
-        for h in range(2):
-            value = held[k][p][side(bit), h].astype(jnp.float32) + got[k][p][h].astype(jnp.float32)
-            store(p, k + 1, h, value)
-        exchange(p, k + 1).start()
-
-    squares = jnp.float32(0.0)
-    for p in sorted(range(count), key=lambda p: pieces[p][3]):
-        which, start, width, _ = pieces[p]
-        k = stages - 1
-        bit = orders[which][1 + k]
-        exchange(p, k).wait_recv()
-        value = held[k][p][side(bit)].astype(jnp.float32) + got[k][p][...].astype(jnp.float32)
-        outs[which][:, start : start + width] = value
-        squares = squares + jnp.sum(value * value)
+        if k < stages_of(p) - 1:
+            for h in range(2):
+                value = held[p][k][mine, h].astype(jnp.float32) + got[p][k][h].astype(jnp.float32)
+                store(p, k + 1, h, value)
+            exchange(p, k + 1).start()
+        else:
+            value = held[p][k][mine].astype(jnp.float32) + got[p][k][...].astype(jnp.float32)
+            outs[which][:, start : start + width] = value
+            squares = squares + jnp.sum(value * value)
 
     sq_send[...] = jnp.full(sq_send.shape, squares, jnp.float32)
 
@@ -329,12 +356,12 @@
         swap(0, part2, other2, i).wait_send()
         swap(1, part_back, other_back, i).wait_send()
     for copy in (
-        send_belief, send_act1, send_act2, send_out, send_slope2, send_slope1,
-        pass_belief, pass_act2, pass_slope2,
+        belief_x, belief_y, relay, *passes, *slopes,
+        send_act1, send_act2, send_out, send_slope2, pass_act2, pass_slope2,
     ):
         copy.wait_send()
     for p in range(count):
-        for k in range(stages):
+        for k in range(stages_of(p)):
             exchange(p, k).wait_send()
     pltpu.make_async_copy(sq_got, sq_got, sq_sems.at[1]).wait()
     everyone = squares + jnp.sum(sq_got[...]) * (1.0 / (sq_send.shape[0] * sq_send.shape[1]))
@@ -352,7 +379,6 @@
 
 def per_device(dims, belief, target_value, counts, w_first, w_middle, w_last):
     n_dp, n_mp = dims
-    stages = n_dp.bit_length() - 2
     blocks = 3
     rows, (in_width, own_hid) = belief.shape[0], w_first.shape
     hid, own_width = w_last.shape
@@ -368,11 +394,14 @@
     pieces = pieces_of(wide)
     half, single = jnp.bfloat16, jnp.float32
 
-    def stage_shape(piece, k):
-        r = long[piece[0]] // 2 >> (k + 1)
-        return (2, r, piece[2]) if k == stages - 1 else (2, 2, r // 2, piece[2])
-
-    shapes = [[stage_shape(piece, k) for piece in pieces] for k in range(stages)]
+    def stage_shapes(piece):
+        shared, rest = orders[piece[0]]
+        for k in range(len(rest)):
+            r = long[piece[0]] >> (len(shared) + k + 1)
+            yield (2, r, piece[2]) if k == len(rest) - 1 else (2, 2, r // 2, piece[2])
+
+    shapes = [list(stage_shapes(piece)) for piece in pieces]
+    deepest = max(len(stages) for stages in shapes)
     loads = (belief.T, target_value.T, w_first, w_middle, w_last.T)
     swapped = pltpu.VMEM((blocks, rows, hid // blocks), single)
     count = len(pieces)
@@ -385,8 +414,8 @@
         + [pl.BlockSpec(memory_space=pl.ANY)] * 5,
         out_specs=[pl.BlockSpec(memory_space=pltpu.VMEM)] * 4,
         scratch_shapes=(
-            [pltpu.VMEM(s, half) for stage in shapes for s in stage]
-            + [pltpu.VMEM(s[1:], half) for stage in shapes for s in stage]
+            [pltpu.VMEM(s, half) for stages in shapes for s in stages]
+            + [pltpu.VMEM(s[1:], half) for stages in shapes for s in stages]
             + [
                 pltpu.VMEM((in_width, rows), half),
                 pltpu.VMEM((n_mp * own_width, rows), half),
@@ -395,10 +424,10 @@
                 pltpu.VMEM((own_width, hid), half),
             ]
             + [pltpu.VMEM((2, 2, long[w] // 4, rows), half) for w in layers]
-            + [pltpu.VMEM((2, long[w] // 4, rows), half) for w in layers]
+            + [pltpu.VMEM((3 if w == FIRST else 2, long[w] // 4, rows), half) for w in layers]
             + [
                 pltpu.VMEM((rows, wide[FIRST]), half),
-                pltpu.VMEM((rows, wide[FIRST]), half),
+                pltpu.VMEM((3, rows, wide[FIRST]), half),
                 pltpu.VMEM((rows, own_hid), single),
                 pltpu.VMEM((rows, own_hid), half),
                 pltpu.VMEM((rows, own_hid), half),
@@ -415,12 +444,12 @@
                 pltpu.SemaphoreType.DMA((5,)),
                 pltpu.SemaphoreType.DMA((2, blocks)),
                 pltpu.SemaphoreType.DMA((2, blocks)),
-                pltpu.SemaphoreType.DMA((9,)),
-                pltpu.SemaphoreType.DMA((9,)),
-                pltpu.SemaphoreType.DMA((stages, count)),
-                pltpu.SemaphoreType.DMA((stages, count)),
-                pltpu.VMEM((8, LANES), single),
-                pltpu.VMEM((n_dp * n_mp - 1, 8, LANES), single),
+                pltpu.SemaphoreType.DMA((15,)),
+                pltpu.SemaphoreType.DMA((15,)),
+                pltpu.SemaphoreType.DMA((count, deepest)),
+                pltpu.SemaphoreType.DMA((count, deepest)),
+                pltpu.VMEM((1, LANES), single),
+                pltpu.VMEM((n_dp * n_mp - 1, 1, LANES), single),
                 pltpu.SemaphoreType.DMA((2,)),
             ]
         ),

time: 90.7 us -> 83.5 us (0.921)
  Pallas kernels: 89.9 us -> 82.7 us
    pallas_call x1, Pallas kernels: 87.6 us -> 80.4 us  [per_device(): pl.pallas_call(functools.partial(step_kernel, dims, params, orders, piece...]
where the time goes in v2:
time: 83.5 us; the launch traced here: 83.3 us
  Pallas kernels  82.7 us (99%)
    pallas_call x1, Pallas kernels, per_device(): pl.pallas_call(functools.partial(step_kernel, dims, params, orders, piece...  80.4 us
    pallas_call x1, Pallas kernels, per_device(): pl.pallas_call(scale_kernel, out_shape=[jax.ShapeDtypeStruct(s, single) f...  2.25 us

profile of v2, /device:TPU:0, one launch (start us, length us, event | category | flops | bytes accessed | tf_op | source)
XLA Modules:
  0.0 83.3 jit_solution(9640311870750260867)
XLA Ops:
  0.6 80.4 %shard_map.85 = (f32[48,2688]{1,0:T(8,128)}, f32[96,768]{1,0:T(8,128)}, f32[96,768]{1,0:T(8,128)}, f32[8,128]{1,0:T(8,128)}) custom-call(s32[2]{0:T(128)} %refs_0_.1, bf16[2652,256]{1,0:T(8,128)(2,1)} %bitcast.6, bf16[1326,256]{1,0:T(8,128)(2,1)} %bitcast.7, bf16[2652,768]{1,0:T(8,128)(2,1)} %refs_3_.1, bf16[768,1536]{1,0:T(8,128)(2,1)} %refs_4_.1, ...), custom_call_target="tpu_custom_call" | custom-call | tf_op jit(solution)/shard_map/pallas_call | solution.py:408
  81.1 2.2 %shard_map.86 = (f32[48,2652]{1,0:T(8,128)}, f32[96,768]{1,0:T(8,128)}, f32[96,663]{1,0:T(8,128)}) custom-call(f32[8,128]{1,0:T(8,128)} %get-tuple-element.10.scale, f32[48,2688]{1,0:T(8,128)} %get-tuple-element.11.refs_0_, f32[96,768]{1,0:T(8,128)} %get-tuple-element.12.refs_1_, f32[96,768]{1,0:T(8,128)} %get-tuple-element.13.refs_2_), custom_call_target="tpu_custom_call" | custom-call | tf_op jit(solution)/shard_map/pallas_call | solution.py:465

commit v3 on v2

v3 whole, which is shorter than its diff:
```python
import functools
import math

import jax
import jax.numpy as jnp
from jax import lax
from jax.experimental import pallas as pl
from jax.experimental.pallas import tpu as pltpu
from jax.sharding import PartitionSpec as P

BLOCK = 128
LANES = 128
MESH = pl.DeviceIdType.MESH
FIRST, MIDDLE, LAST = 0, 1, 2
NT = (((1,), (1,)), ((), ()))


def silu_slope(pre_act):
    sigmoid_of = jax.nn.sigmoid(pre_act)
    return sigmoid_of * (1.0 + pre_act * (1.0 - sigmoid_of))


def pad_to(size, step):
    return -(-size // step) * step


SHARED = {FIRST: (0, 1), MIDDLE: (2,), LAST: (2,)}
PIECES = (
    (LAST, (0, 1), 1, 25.3, (30.1, 35.2, 50)),
    (LAST, (1, 0), 1, 25.4, (30.2, 35.3, 50.1)),
    (LAST, (0, 1), 2, 25.5, (34.2, 38.2, 53)),
    (LAST, (1, 0), 2, 25.6, (34.3, 38.3, 53.1)),
    (FIRST, (2,), 5, 18.8, (27.8, 48)),
    (FIRST, (2,), 5, 25.9, (34.6, 49)),
    (FIRST, (2,), 5, 27.8, (37.5, 51)),
    (FIRST, (2,), 6, 29.6, (40.4, 52)),
    (MIDDLE, (1, 0), 1, 33.6, (37.4, 43.3, 54)),
    (MIDDLE, (0, 1), 1, 33.7, (37.41, 43.4, 54.1)),
    (MIDDLE, (1, 0), 2, 34.5, (42.3, 46.2, 55)),
    (MIDDLE, (0, 1), 2, 34.6, (42.4, 46.3, 55.1)),
)


def pieces_of(n_dp, wide):
    total = n_dp.bit_length() - 1
    out = []
    for which in (LAST, FIRST, MIDDLE):
        mine = [piece for piece in PIECES if piece[0] == which]
        tiles, parts = wide[which] // LANES, [piece[2] for piece in mine]
        bounds = [
            round(tiles * sum(parts[:i]) / sum(parts)) * LANES for i in range(len(mine) + 1)
        ]
        for i, (_, head, _, when, keys) in enumerate(mine):
            tail = [b for b in range(total) if b not in SHARED[which] + head]
            bits = head + tuple(tail)
            more = len(bits) - len(keys)
            keys = keys[:-1] + tuple(keys[-2] + 7 * (j + 1) for j in range(more)) + (keys[-1] + 7 * more,)
            out.append((which, bounds[i], bounds[i + 1] - bounds[i], bits, when, keys))
    return out


def step_kernel(dims, params, pieces, stage_shapes, *refs):
    n_dp, n_mp = dims
    count = len(pieces)
    counts, loads, outs, scale_out = refs[0], refs[1:6], refs[6:9], refs[9]
    refs = refs[10:]
    held, got = [], []
    for group in (held, got):
        for shapes in stage_shapes:
            group.append(refs[: len(shapes)])
            refs = refs[len(shapes) :]
    finals, refs = refs[:count], refs[count:]
    belief_t, target_t, w_first, w_middle, w_last_t = refs[:5]
    parts_t, near_t = refs[5:8], refs[8:11]
    (
        belief, near_belief, pre1, act1, near_act1, part2, other2, pre2, act2, slope_out, near_out,
        part_back, other_back, slope2, slope1, load_sems, swap_send, swap_got, share_send, share_got,
        sends, gots, leave_sems, sq_send, sq_got, sq_sems,
    ) = refs[11:]

    in_width, own_hid = w_first.shape
    own_width, hid = w_last_t.shape
    rows = belief.shape[0]
    blocks = part2.shape[0]
    block = hid // blocks

    landing = (belief_t, target_t, w_first, w_middle, w_last_t)
    arrivals = [
        pltpu.make_async_copy(src, dst, load_sems.at[i])
        for i, (src, dst) in enumerate(zip(loads, landing))
    ]
    arrivals[0].start()

    dp, mp = lax.axis_index("dp"), lax.axis_index("mp")
    me = dp * n_mp + mp
    total = n_dp * n_mp

    def side(bit):
        return (dp // (1 << bit)) % 2

    def peer(bit):
        return (dp + (1 - 2 * side(bit)) * (1 << bit), mp)

    sibling = (dp, 1 - mp)
    x, y = (side(bit) for bit in SHARED[FIRST])
    x_peer, y_peer = (peer(bit) for bit in SHARED[FIRST])
    diagonal = (x_peer[0] + y_peer[0] - dp, mp)
    (low,) = SHARED[MIDDLE]
    z, z_peer = side(low), peer(low)
    bits = n_dp.bit_length() - 1
    partners = [sibling, diagonal] + [peer(bit) for bit in range(bits)]
    barrier = pltpu.get_barrier_semaphore()
    for partner in partners:
        pl.semaphore_signal(barrier, inc=1, device_id=partner, device_id_type=MESH)
    for i in (2, 3, 4, 1):
        arrivals[i].start()

    def remote(src, dst, sems, k, goal):
        return pltpu.make_async_remote_copy(
            src, dst, sems[0].at[k], sems[1].at[k], device_id=goal, device_id_type=MESH
        )

    share = functools.partial(remote, sems=(share_send, share_got))
    own_shares = 9
    my_rows = pl.ds(pl.multiple_of(mp * (rows // 2), rows // 2), rows // 2)
    relay_goal = (jnp.where(mp == 0, y_peer[0], x_peer[0]), mp)
    bands = [pl.ds(piece[1], piece[2]) for piece in pieces if piece[0] == FIRST]
    nears = []
    for i, goal in enumerate((x_peer, y_peer)):
        nears.append([
            share(
                belief.at[my_rows, band], near_belief.at[i, my_rows, band],
                k=own_shares + 6 * c + i, goal=goal,
            )
            for c, band in enumerate(bands)
        ])
    relays = [
        share(
            near_belief.at[mp, my_rows, band], near_belief.at[2, my_rows, band],
            k=own_shares + 6 * c + 2, goal=relay_goal,
        )
        for c, band in enumerate(bands)
    ]
    passes = [
        [
            share(
                near_belief.at[i, my_rows, band], near_belief.at[i, my_rows, band],
                k=own_shares + 6 * c + 3 + i, goal=sibling,
            )
            for i in range(3)
        ]
        for c, band in enumerate(bands)
    ]
    slopes = [
        share(parts_t[FIRST].at[at], near_t[FIRST].at[i], k=i, goal=goal)
        for i, (at, goal) in enumerate(
            (((1 - x, y), x_peer), ((x, 1 - y), y_peer), ((1 - x, 1 - y), diagonal))
        )
    ]
    send_act1 = share(act1, near_act1, k=3, goal=z_peer)
    send_act2 = share(parts_t[LAST].at[1 - z, mp], near_t[LAST].at[mp], k=4, goal=z_peer)
    send_out = share(slope_out, near_out, k=5, goal=z_peer)
    send_slope2 = share(parts_t[MIDDLE].at[1 - z, mp], near_t[MIDDLE].at[mp], k=6, goal=z_peer)
    pass_act2 = share(near_t[LAST].at[mp], near_t[LAST].at[mp], k=7, goal=sibling)
    pass_slope2 = share(near_t[MIDDLE].at[mp], near_t[MIDDLE].at[mp], k=8, goal=sibling)

    def swap(way, part, other, i):
        return pltpu.make_async_remote_copy(
            part.at[i], other.at[i], swap_send.at[way, i], swap_got.at[way, i],
            device_id=sibling, device_id_type=MESH,
        )

    def transpose_parts(which, source, width):
        order = SHARED[which] + tuple(b for b in range(bits) if b not in SHARED[which])
        r = width // n_dp
        step = math.lcm(r, LANES)
        for start in range(0, width, step):
            value = source[:, start : start + step].T
            for d in range(start // r, (start + step) // r):
                where = [(d >> bit) & 1 for bit in order]
                at = 0
                for bit in where[2:]:
                    at = 2 * at + bit
                parts_t[which][where[0], where[1], at * r : (at + 1) * r, :] = value[
                    d * r - start : (d + 1) * r - start
                ]

    def leave(p):
        which, start, width = pieces[p][:3]
        return pltpu.make_async_copy(
            finals[p], outs[which].at[:, pl.ds(start, width)], leave_sems.at[p]
        )

    def dot(left, right):
        return jnp.dot(left, right, preferred_element_type=jnp.float32)

    def first_grad(p):
        start, width = pieces[p][1:3]
        cols = slice(start, start + width)
        value = dot(parts_t[FIRST][x, y], belief[:, cols])
        for i in range(3):
            value = value + dot(near_t[FIRST][i], near_belief[i, :, cols])
        h = value.shape[0] // 2
        store(p, 0, 0, value[:h])
        store(p, 0, 1, value[h:])
        exchange(p, 0).start()

    rights = {MIDDLE: (act1, near_act1), LAST: (slope_out, near_out)}

    def half_grad(p, half):
        which, start, width, order, _, _ = pieces[p]
        own, near = rights[which]
        cols = slice(start, start + width)
        value = dot(parts_t[which][z, half], own[:, cols]) + dot(near_t[which][half], near[:, cols])
        if order[0] == 0:
            store(p, 0, half, value)
        else:
            h = value.shape[0] // 2
            held[p][0][0, half] = value[:h].astype(jnp.bfloat16)
            held[p][0][1, half] = value[h:].astype(jnp.bfloat16)

    def grad(p):
        if pieces[p][0] == FIRST:
            first_grad(p)
        elif pieces[p][3][0] == 0:
            half_grad(p, 1 - x)
            exchange(p, 0).start()
            half_grad(p, x)
        else:
            half_grad(p, 0)
            half_grad(p, 1)
            exchange(p, 0).start()

    def stages_of(p):
        return len(pieces[p][3])

    def store(p, k, half, value):
        ref = held[p][k]
        if k == stages_of(p) - 1:
            ref[half] = value.astype(jnp.bfloat16)
            return
        h = value.shape[0] // 2
        ref[half, 0] = value[:h].astype(jnp.bfloat16)
        ref[half, 1] = value[h:].astype(jnp.bfloat16)

    def exchange(p, k):
        bit = pieces[p][3][k]
        return pltpu.make_async_remote_copy(
            held[p][k].at[1 - side(bit)], got[p][k], sends.at[p, k], gots.at[p, k],
            device_id=peer(bit), device_id_type=MESH,
        )

    def turn(got_first, then):
        for copy in got_first:
            copy.wait_recv()
        for copy in then:
            copy.start()

    def hand_on(c):
        turn((nears[0][c], nears[1][c]), (relays[c], passes[c][0], passes[c][1]))

    arrivals[0].wait()
    for start in range(0, belief.shape[1], LANES * 3):
        value = belief_t[start : min(start + LANES * 3, in_width), :]
        if value.shape[0] < LANES * 3:
            value = jnp.concatenate(
                [value, jnp.zeros((LANES * 3 - value.shape[0], rows), jnp.bfloat16)], axis=0
            )
        belief[:, start : start + LANES * 3] = value.T
    pl.semaphore_wait(barrier, len(partners))
    early = len(bands) - 1
    for c in range(early):
        nears[0][c].start()
        nears[1][c].start()
    arrivals[2].wait()
    for c in range(0, own_hid, 256):
        value = jnp.dot(
            belief[:, :in_width], w_first[:, c : c + 256], preferred_element_type=jnp.float32
        )
        pre1[:, c : c + 256] = value
        act1[:, c : c + 256] = jax.nn.silu(value).astype(jnp.bfloat16)
    send_act1.start()
    arrivals[3].wait()
    for i in range(blocks):
        part2[i] = jnp.dot(
            act1[...], w_middle[:, i * block : (i + 1) * block],
            preferred_element_type=jnp.float32,
        )
        swap(0, part2, other2, i).start()
    arrivals[1].wait()
    arrivals[4].wait()
    row = lax.broadcasted_iota(jnp.int32, (rows, 1), 0)
    limit = jnp.full((rows, 1), counts[0], jnp.int32)
    for b in range(1, rows // BLOCK):
        limit = jnp.where(row >= b * BLOCK, counts[b] + b * BLOCK, limit)
    live = jnp.where(row < limit, 1.0, 0.0)
    target = target_t[...].T
    wanted = target[:, :own_width].astype(jnp.float32)
    for m in range(1, n_mp):
        wanted = jnp.where(
            mp == m, target[:, m * own_width : (m + 1) * own_width].astype(jnp.float32), wanted
        )
    for i in range(blocks):
        cols = slice(i * block, (i + 1) * block)
        swap(0, part2, other2, i).wait_recv()
        value = part2[i] + other2[i]
        pre2[:, cols] = value
        act2[:, cols] = jax.nn.silu(value).astype(jnp.bfloat16)
    transpose_parts(LAST, act2, hid)
    send_act2.start()
    predicted = lax.dot_general(act2[...], w_last_t[...], NT, preferred_element_type=jnp.float32)
    value = jnp.clip(predicted - wanted, -1.0, 1.0) * live
    slope_out[...] = jnp.concatenate(
        [value, jnp.zeros((rows, slope_out.shape[1] - own_width), jnp.float32)], axis=1
    ).astype(jnp.bfloat16)
    send_out.start()
    hand_on(0)

    for i in range(blocks):
        part_back[i] = jnp.dot(
            slope_out[:, :own_width], w_last_t[:, i * block : (i + 1) * block],
            preferred_element_type=jnp.float32,
        )
        swap(1, part_back, other_back, i).start()
    for i in range(blocks):
        cols = slice(i * block, (i + 1) * block)
        swap(1, part_back, other_back, i).wait_recv()
        value = (part_back[i] + other_back[i]) * silu_slope(pre2[:, cols])
        slope2[:, cols] = value.astype(jnp.bfloat16)
    transpose_parts(MIDDLE, slope2, hid)
    for c in range(0, own_hid, 256):
        back = lax.dot_general(
            slope2[...], w_middle[c : c + 256, :], NT, preferred_element_type=jnp.float32
        )
        slope1[:, c : c + 256] = (back * silu_slope(pre1[:, c : c + 256])).astype(jnp.bfloat16)
    transpose_parts(FIRST, slope1, own_hid)
    for copy in slopes:
        copy.start()
    for c in range(early, len(bands)):
        nears[0][c].start()
        nears[1][c].start()

    def step(p, k):
        mine = side(pieces[p][3][k])
        exchange(p, k).wait_recv()
        for h in range(2):
            value = held[p][k][mine, h].astype(jnp.float32) + got[p][k][h].astype(jnp.float32)
            store(p, k + 1, h, value)
        exchange(p, k + 1).start()

    def finish(p, k):
        mine = side(pieces[p][3][k])
        exchange(p, k).wait_recv()
        value = held[p][k][mine].astype(jnp.float32) + got[p][k][...].astype(jnp.float32)
        finals[p][...] = value
        leave(p).start()
        across = jnp.sum(value * value, axis=0, keepdims=True)
        for start in range(0, value.shape[1], LANES):
            squares.append(across[:, start : start + LANES])

    squares = []
    actions = [
        (15, turn, ([relays[0]], [passes[0][2]])),
        (16.8, turn, ([send_act2], [pass_act2])),
        (18.7, turn, (slopes + passes[0], [])),
        (18.9, turn, ([], [send_slope2])),
        (25.2, turn, ([pass_act2, send_out], [])),
        (31.9, turn, ([send_slope2], [pass_slope2])),
        (33.5, turn, ([send_act1, pass_slope2], [])),
    ]
    for c in range(1, len(bands)):
        seen = 12.1 + 0.6 * c if c < early else 22.4
        actions.append((seen, hand_on, (c,)))
        actions.append((22.2 + 1.9 * c, turn, ([relays[c]], [passes[c][2]])))
        actions.append((23.9 + 1.9 * c, turn, (passes[c], [])))
    for p in range(count):
        actions.append((pieces[p][4], grad, (p,)))
        for k in range(stages_of(p)):
            does = step if k < stages_of(p) - 1 else finish
            actions.append((pieces[p][5][k], does, (p, k)))
    for _, does, what in sorted(actions, key=lambda action: action[0]):
        does(*what)
    squares = jnp.sum(sum(squares[1:], squares[0]), axis=1, keepdims=True)

    sq_send[...] = jnp.broadcast_to(squares, sq_send.shape)

    def square_copy(j):
        other = lax.rem(me + j, total)
        return pltpu.make_async_remote_copy(
            sq_send, sq_got.at[j - 1], sq_sems.at[0], sq_sems.at[1],
            device_id=(other // n_mp, other % n_mp), device_id_type=MESH,
        )

    def tell(j, _):
        square_copy(j).start()
        return 0

    lax.fori_loop(1, total, tell, 0)
    for i in range(blocks):
        swap(0, part2, other2, i).wait_send()
        swap(1, part_back, other_back, i).wait_send()
    for copy in (
        *nears[0], *nears[1], *relays, *sum(passes, []), *slopes,
        send_act1, send_act2, send_out, send_slope2, pass_act2, pass_slope2,
    ):
        copy.wait_send()
    for p in range(count):
        for k in range(stages_of(p)):
            exchange(p, k).wait_send()
        leave(p).wait()
    pltpu.make_async_copy(sq_got, sq_got, sq_sems.at[1]).wait()
    everyone = squares + jnp.sum(sq_got[...], axis=0)
    scale_out[...] = jnp.broadcast_to(lax.rsqrt(everyone / params + 1e-06), scale_out.shape)
    pltpu.make_async_copy(sq_got, sq_got, sq_sems.at[0]).wait()


def scale_kernel(scale, *refs):
    factor = scale[0:1, 0:1]
    for raw, out in zip(refs[:3], refs[3:]):
        out[...] = raw[:, : out.shape[1]] * factor


def per_device(dims, belief, target_value, counts, w_first, w_middle, w_last):
    n_dp, n_mp = dims
    blocks = 3
    rows, (in_width, own_hid) = belief.shape[0], w_first.shape
    hid, own_width = w_last.shape
    params = float(n_mp * (w_first.size + w_middle.size + w_last.size))
    long = {FIRST: own_hid, MIDDLE: hid, LAST: hid}
    wide = {
        FIRST: pad_to(in_width, LANES),
        MIDDLE: pad_to(own_hid, LANES),
        LAST: pad_to(own_width, LANES),
    }
    layers = (FIRST, MIDDLE, LAST)
    pieces = pieces_of(n_dp, wide)
    half, single = jnp.bfloat16, jnp.float32

    def stage_shapes(piece):
        stages = len(piece[3])
        for k in range(stages):
            r = long[piece[0]] >> (len(SHARED[piece[0]]) + k + 1)
            yield (2, r, piece[2]) if k == stages - 1 else (2, 2, r // 2, piece[2])

    shapes = [list(stage_shapes(piece)) for piece in pieces]
    shares = 9 + 6 * sum(piece[0] == FIRST for piece in pieces)
    deepest = max(len(stages) for stages in shapes)
    loads = (belief.T, target_value.T, w_first, w_middle, w_last.T)
    swapped = pltpu.VMEM((blocks, rows, hid // blocks), single)
    count = len(pieces)
    raws = pl.pallas_call(
        functools.partial(step_kernel, dims, params, pieces, shapes),
        out_shape=[
            jax.ShapeDtypeStruct((long[w] // n_dp, wide[w]), single) for w in layers
        ] + [jax.ShapeDtypeStruct((8, LANES), single)],
        in_specs=[pl.BlockSpec(memory_space=pltpu.SMEM)]
        + [pl.BlockSpec(memory_space=pl.ANY)] * 5,
        out_specs=[pl.BlockSpec(memory_space=pl.ANY)] * 3
        + [pl.BlockSpec(memory_space=pltpu.VMEM)],
        scratch_shapes=(
            [pltpu.VMEM(s, half) for stages in shapes for s in stages]
            + [pltpu.VMEM(s[1:], half) for stages in shapes for s in stages]
            + [pltpu.VMEM(stages[-1][1:], single) for stages in shapes]
            + [
                pltpu.VMEM((in_width, rows), half),
                pltpu.VMEM((n_mp * own_width, rows), half),
                pltpu.VMEM(w_first.shape, half),
                pltpu.VMEM(w_middle.shape, half),
                pltpu.VMEM((own_width, hid), half),
            ]
            + [pltpu.VMEM((2, 2, long[w] // 4, rows), half) for w in layers]
            + [pltpu.VMEM((3 if w == FIRST else 2, long[w] // 4, rows), half) for w in layers]
            + [
                pltpu.VMEM((rows, wide[FIRST]), half),
                pltpu.VMEM((3, rows, wide[FIRST]), half),
                pltpu.VMEM((rows, own_hid), single),
                pltpu.VMEM((rows, own_hid), half),
                pltpu.VMEM((rows, own_hid), half),
                swapped,
                swapped,
                pltpu.VMEM((rows, hid), single),
                pltpu.VMEM((rows, hid), half),
                pltpu.VMEM((rows, wide[LAST]), half),
                pltpu.VMEM((rows, wide[LAST]), half),
                swapped,
                swapped,
                pltpu.VMEM((rows, hid), half),
                pltpu.VMEM((rows, own_hid), half),
                pltpu.SemaphoreType.DMA((5,)),
                pltpu.SemaphoreType.DMA((2, blocks)),
                pltpu.SemaphoreType.DMA((2, blocks)),
                pltpu.SemaphoreType.DMA((shares,)),
                pltpu.SemaphoreType.DMA((shares,)),
                pltpu.SemaphoreType.DMA((count, deepest)),
                pltpu.SemaphoreType.DMA((count, deepest)),
                pltpu.SemaphoreType.DMA((count,)),
                pltpu.VMEM((1, LANES), single),
                pltpu.VMEM((n_dp * n_mp - 1, 1, LANES), single),
                pltpu.SemaphoreType.DMA((2,)),
            ]
        ),
        compiler_params=pltpu.CompilerParams(
            collective_id=0, has_side_effects=True, vmem_limit_bytes=60 * 1024 * 1024
        ),
    )(counts, *loads)
    ends = (
        (long[FIRST] // n_dp, in_width),
        (long[MIDDLE] // n_dp, own_hid),
        (long[LAST] // n_dp, own_width),
    )
    first, middle, last = pl.pallas_call(
        scale_kernel,
        out_shape=[jax.ShapeDtypeStruct(s, single) for s in ends],
        in_specs=[pl.BlockSpec(memory_space=pltpu.VMEM)] * 4,
        out_specs=[pl.BlockSpec(memory_space=pltpu.VMEM)] * 3,
    )(raws[3], *raws[:3])
    return first.T, middle.T, last


def solution(mesh):
    return jax.shard_map(
        functools.partial(per_device, (mesh.shape["dp"], mesh.shape["mp"])),
        mesh=mesh,
        in_specs=(
            P("dp", None),
            P("dp", None),
            P("dp"),
            P(None, "mp"),
            P("mp", None),
            P(None, "mp"),
        ),
        out_specs=(P(None, ("mp", "dp")), P("mp", "dp"), P("dp", "mp")),
        check_vma=False,
    )
```

time: 83.5 us -> 75.6 us (0.905)
  Pallas kernels: 82.7 us -> 74.9 us
    pallas_call x1, Pallas kernels: 80.4 us -> 72.6 us  [per_device(): pl.pallas_call(functools.partial(step_kernel, dims, params, pieces, shape...]
where the time goes in v3:
time: 75.6 us; the launch traced here: 75.5 us
  Pallas kernels  74.9 us (99%)
    pallas_call x1, Pallas kernels, per_device(): pl.pallas_call(functools.partial(step_kernel, dims, params, pieces, shape...  72.6 us
    pallas_call x1, Pallas kernels, per_device(): pl.pallas_call(scale_kernel, out_shape=[jax.ShapeDtypeStruct(s, single) f...  2.25 us

profile of v3, /device:TPU:0, one launch (start us, length us, event | category | flops | bytes accessed | tf_op | source)
XLA Modules:
  0.0 75.5 jit_solution(7140758621423654728)
XLA Ops:
  0.6 72.6 %shard_map.85 = (f32[48,2688]{1,0:T(8,128)}, f32[96,768]{1,0:T(8,128)}, f32[96,768]{1,0:T(8,128)}, f32[8,128]{1,0:T(8,128)}) custom-call(s32[2]{0:T(128)} %refs_0_.1, bf16[2652,256]{1,0:T(8,128)(2,1)} %bitcast.6, bf16[1326,256]{1,0:T(8,128)(2,1)} %bitcast.7, bf16[2652,768]{1,0:T(8,128)(2,1)} %refs_3_.1, bf16[768,1536]{1,0:T(8,128)(2,1)} %refs_4_.1, ...), custom_call_target="tpu_custom_call" | custom-call | tf_op jit(solution)/shard_map/pallas_call | solution.py:451
  73.2 2.2 %shard_map.86 = (f32[48,2652]{1,0:T(8,128)}, f32[96,768]{1,0:T(8,128)}, f32[96,663]{1,0:T(8,128)}) custom-call(f32[8,128]{1,0:T(8,128)} %get-tuple-element.10.scale, f32[48,2688]{1,0:T(8,128)} %get-tuple-element.11.refs_0_, f32[96,768]{1,0:T(8,128)} %get-tuple-element.12.refs_1_, f32[96,768]{1,0:T(8,128)} %get-tuple-element.13.refs_2_), custom_call_target="tpu_custom_call" | custom-call | tf_op jit(solution)/shard_map/pallas_call | solution.py:511

commit v4 on v3

--- a/solution.py
+++ b/solution.py
@@ -24,20 +24,20 @@
     return -(-size // step) * step
 
 
-SHARED = {FIRST: (0, 1), MIDDLE: (2,), LAST: (2,)}
+SHARED = {FIRST: (0, 1), MIDDLE: (2,), LAST: (3,)}
 PIECES = (
-    (LAST, (0, 1), 1, 25.3, (30.1, 35.2, 50)),
-    (LAST, (1, 0), 1, 25.4, (30.2, 35.3, 50.1)),
-    (LAST, (0, 1), 2, 25.5, (34.2, 38.2, 53)),
-    (LAST, (1, 0), 2, 25.6, (34.3, 38.3, 53.1)),
-    (FIRST, (2,), 5, 18.8, (27.8, 48)),
-    (FIRST, (2,), 5, 25.9, (34.6, 49)),
-    (FIRST, (2,), 5, 27.8, (37.5, 51)),
-    (FIRST, (2,), 6, 29.6, (40.4, 52)),
-    (MIDDLE, (1, 0), 1, 33.6, (37.4, 43.3, 54)),
-    (MIDDLE, (0, 1), 1, 33.7, (37.41, 43.4, 54.1)),
-    (MIDDLE, (1, 0), 2, 34.5, (42.3, 46.2, 55)),
-    (MIDDLE, (0, 1), 2, 34.6, (42.4, 46.3, 55.1)),
+    (LAST, (0, 1), 1, 34.4, (38.2, 43.4, 53)),
+    (LAST, (1, 0), 1, 34.5, (38.3, 43.5, 53.1)),
+    (LAST, (0, 1), 2, 34.6, (42.4, 46.2, 54)),
+    (LAST, (1, 0), 2, 34.7, (42.5, 46.3, 54.1)),
+    (FIRST, (2,), 5, 18.8, (36.2, 50)),
+    (FIRST, (2,), 5, 25.9, (38.7, 50.1)),
+    (FIRST, (2,), 5, 27.8, (41.4, 51)),
+    (FIRST, (2,), 6, 29.6, (44.6, 52)),
+    (MIDDLE, (1, 0), 1, 27, (30.8, 36, 49)),
+    (MIDDLE, (0, 1), 1, 27.1, (30.9, 36.1, 49.1)),
+    (MIDDLE, (1, 0), 2, 27.2, (35, 38.8, 50.5)),
+    (MIDDLE, (0, 1), 2, 27.3, (35.1, 38.9, 50.6)),
 )
 
 
@@ -105,8 +105,8 @@
     x, y = (side(bit) for bit in SHARED[FIRST])
     x_peer, y_peer = (peer(bit) for bit in SHARED[FIRST])
     diagonal = (x_peer[0] + y_peer[0] - dp, mp)
-    (low,) = SHARED[MIDDLE]
-    z, z_peer = side(low), peer(low)
+    pair_side = {which: side(SHARED[which][0]) for which in (MIDDLE, LAST)}
+    pair_peer = {which: peer(SHARED[which][0]) for which in (MIDDLE, LAST)}
     bits = n_dp.bit_length() - 1
     partners = [sibling, diagonal] + [peer(bit) for bit in range(bits)]
     barrier = pltpu.get_barrier_semaphore()
@@ -157,10 +157,15 @@
             (((1 - x, y), x_peer), ((x, 1 - y), y_peer), ((1 - x, 1 - y), diagonal))
         )
     ]
-    send_act1 = share(act1, near_act1, k=3, goal=z_peer)
-    send_act2 = share(parts_t[LAST].at[1 - z, mp], near_t[LAST].at[mp], k=4, goal=z_peer)
-    send_out = share(slope_out, near_out, k=5, goal=z_peer)
-    send_slope2 = share(parts_t[MIDDLE].at[1 - z, mp], near_t[MIDDLE].at[mp], k=6, goal=z_peer)
+    send_act1 = share(act1, near_act1, k=3, goal=pair_peer[MIDDLE])
+    send_act2 = share(
+        parts_t[LAST].at[1 - pair_side[LAST], mp], near_t[LAST].at[mp], k=4, goal=pair_peer[LAST]
+    )
+    send_out = share(slope_out, near_out, k=5, goal=pair_peer[LAST])
+    send_slope2 = share(
+        parts_t[MIDDLE].at[1 - pair_side[MIDDLE], mp], near_t[MIDDLE].at[mp], k=6,
+        goal=pair_peer[MIDDLE],
+    )
     pass_act2 = share(near_t[LAST].at[mp], near_t[LAST].at[mp], k=7, goal=sibling)
     pass_slope2 = share(near_t[MIDDLE].at[mp], near_t[MIDDLE].at[mp], k=8, goal=sibling)
 
@@ -211,7 +216,8 @@
         which, start, width, order, _, _ = pieces[p]
         own, near = rights[which]
         cols = slice(start, start + width)
-        value = dot(parts_t[which][z, half], own[:, cols]) + dot(near_t[which][half], near[:, cols])
+        value = dot(parts_t[which][pair_side[which], half], own[:, cols])
+        value = value + dot(near_t[which][half], near[:, cols])
         if order[0] == 0:
             store(p, 0, half, value)
         else:
@@ -313,7 +319,6 @@
     slope_out[...] = jnp.concatenate(
         [value, jnp.zeros((rows, slope_out.shape[1] - own_width), jnp.float32)], axis=1
     ).astype(jnp.bfloat16)
-    send_out.start()
     hand_on(0)
 
     for i in range(blocks):
@@ -328,6 +333,7 @@
         value = (part_back[i] + other_back[i]) * silu_slope(pre2[:, cols])
         slope2[:, cols] = value.astype(jnp.bfloat16)
     transpose_parts(MIDDLE, slope2, hid)
+    send_slope2.start()
     for c in range(0, own_hid, 256):
         back = lax.dot_general(
             slope2[...], w_middle[c : c + 256, :], NT, preferred_element_type=jnp.float32
@@ -361,12 +367,12 @@
     squares = []
     actions = [
         (15, turn, ([relays[0]], [passes[0][2]])),
-        (16.8, turn, ([send_act2], [pass_act2])),
         (18.7, turn, (slopes + passes[0], [])),
-        (18.9, turn, ([], [send_slope2])),
-        (25.2, turn, ([pass_act2, send_out], [])),
-        (31.9, turn, ([send_slope2], [pass_slope2])),
-        (33.5, turn, ([send_act1, pass_slope2], [])),
+        (11.9, turn, ([], [send_out])),
+        (21.8, turn, ([send_act2], [pass_act2])),
+        (25.3, turn, ([send_slope2], [pass_slope2])),
+        (26.9, turn, ([send_act1, pass_slope2], [])),
+        (34.3, turn, ([pass_act2, send_out], [])),
     ]
     for c in range(1, len(bands)):
         seen = 12.1 + 0.6 * c if c < early else 22.4

time: 75.6 us -> 72.5 us (0.959)
  Pallas kernels: 74.9 us -> 71.7 us
    pallas_call x1, Pallas kernels: 72.6 us -> 69.5 us  [per_device(): pl.pallas_call(functools.partial(step_kernel, dims, params, pieces, shape...]
where the time goes in v4:
time: 72.5 us; the launch traced here: 72.3 us
  Pallas kernels  71.7 us (99%)
    pallas_call x1, Pallas kernels, per_device(): pl.pallas_call(functools.partial(step_kernel, dims, params, pieces, shape...  69.5 us
    pallas_call x1, Pallas kernels, per_device(): pl.pallas_call(scale_kernel, out_shape=[jax.ShapeDtypeStruct(s, single) f...  2.25 us

profile of v4, /device:TPU:0, one launch (start us, length us, event | category | flops | bytes accessed | tf_op | source)
XLA Modules:
  0.0 72.3 jit_solution(9443789787715577399)
XLA Ops:
  0.6 69.5 %shard_map.85 = (f32[48,2688]{1,0:T(8,128)}, f32[96,768]{1,0:T(8,128)}, f32[96,768]{1,0:T(8,128)}, f32[8,128]{1,0:T(8,128)}) custom-call(s32[2]{0:T(128)} %refs_0_.1, bf16[2652,256]{1,0:T(8,128)(2,1)} %bitcast.6, bf16[1326,256]{1,0:T(8,128)(2,1)} %bitcast.7, bf16[2652,768]{1,0:T(8,128)(2,1)} %refs_3_.1, bf16[768,1536]{1,0:T(8,128)(2,1)} %refs_4_.1, ...), custom_call_target="tpu_custom_call" | custom-call | tf_op jit(solution)/shard_map/pallas_call | solution.py:457
  70.1 2.2 %shard_map.86 = (f32[48,2652]{1,0:T(8,128)}, f32[96,768]{1,0:T(8,128)}, f32[96,663]{1,0:T(8,128)}) custom-call(f32[8,128]{1,0:T(8,128)} %get-tuple-element.10.scale, f32[48,2688]{1,0:T(8,128)} %get-tuple-element.11.refs_0_, f32[96,768]{1,0:T(8,128)} %get-tuple-element.12.refs_1_, f32[96,768]{1,0:T(8,128)} %get-tuple-element.13.refs_2_), custom_call_target="tpu_custom_call" | custom-call | tf_op jit(solution)/shard_map/pallas_call | solution.py:517

commit v5 on v4

--- a/solution.py
+++ b/solution.py
@@ -390,18 +390,16 @@
 
     sq_send[...] = jnp.broadcast_to(squares, sq_send.shape)
 
-    def square_copy(j):
-        other = lax.rem(me + j, total)
-        return pltpu.make_async_remote_copy(
-            sq_send, sq_got.at[j - 1], sq_sems.at[0], sq_sems.at[1],
-            device_id=(other // n_mp, other % n_mp), device_id_type=MESH,
-        )
-
-    def tell(j, _):
-        square_copy(j).start()
-        return 0
-
-    lax.fori_loop(1, total, tell, 0)
+    k = 0
+    for shift in range(n_dp - 1, -1, -1):
+        chip = dp + shift
+        chip = jnp.where(chip >= n_dp, chip - n_dp, chip)
+        for core in (mp, 1 - mp) if shift else (1 - mp,):
+            pltpu.make_async_remote_copy(
+                sq_send, sq_got.at[k], sq_sems.at[0], sq_sems.at[1],
+                device_id=(chip, core), device_id_type=MESH,
+            ).start()
+            k += 1
     for i in range(blocks):
         swap(0, part2, other2, i).wait_send()
         swap(1, part_back, other_back, i).wait_send()
@@ -506,7 +504,7 @@
             ]
         ),
         compiler_params=pltpu.CompilerParams(
-            collective_id=0, has_side_effects=True, vmem_limit_bytes=60 * 1024 * 1024
+            collective_id=0, has_side_effects=True, vmem_limit_bytes=105 * 512 * 1024
         ),
     )(counts, *loads)
     ends = (
@@ -519,6 +517,7 @@
         out_shape=[jax.ShapeDtypeStruct(s, single) for s in ends],
         in_specs=[pl.BlockSpec(memory_space=pltpu.VMEM)] * 4,
         out_specs=[pl.BlockSpec(memory_space=pltpu.VMEM)] * 3,
+        compiler_params=pltpu.CompilerParams(vmem_limit_bytes=4 * 1024 * 1024),
     )(raws[3], *raws[:3])
     return first.T, middle.T, last
 

time: 72.5 us -> 71.4 us (0.985)
  Pallas kernels: 71.7 us -> 70 us
    pallas_call x1, Pallas kernels: 2.25 us -> 1.04 us  [per_device(): pl.pallas_call(scale_kernel, out_shape=[jax.ShapeDtypeStruct(s, single) f...]
where the time goes in v5:
time: 71.4 us; the launch traced here: 71.3 us
  Pallas kernels  70 us (98%)
    pallas_call x1, Pallas kernels, per_device(): pl.pallas_call(functools.partial(step_kernel, dims, params, pieces, shape...  68.9 us

profile of v5, /device:TPU:0, one launch (start us, length us, event | category | flops | bytes accessed | tf_op | source)
XLA Modules:
  0.0 71.3 jit_solution(13718699781468501580)
XLA Ops:
  0.6 0.0 copy-start
  0.6 0.6 copy-done
  1.3 68.9 %shard_map.85 = (f32[48,2688]{1,0:T(8,128)S(1)}, f32[96,768]{1,0:T(8,128)S(1)}, f32[96,768]{1,0:T(8,128)S(1)}, f32[8,128]{1,0:T(8,128)S(1)}) custom-call(s32[2]{0:T(128)S(1)} %copy-done, bf16[2652,256]{1,0:T(8,128)(2,1)} %bitcast.6, bf16[1326,256]{1,0:T(8,128)(2,1)} %bitcast.7, bf16[2652,768]{1,0:T(8,128)(2,1)} %refs_3_.1, bf16[768,1536]{1,0:T(8,128)(2,1)} %refs_4_.1, ...), custom_call_target="tpu_custom_call" | custom-call | tf_op jit(solution)/shard_map/pallas_call | solution.py:455
  70.2 1.0 %shard_map.86 = (f32[48,2652]{1,0:T(8,128)}, f32[96,768]{1,0:T(8,128)}, f32[96,663]{1,0:T(8,128)}) custom-call(f32[8,128]{1,0:T(8,128)S(1)} %get-tuple-element.10.scale, f32[48,2688]{1,0:T(8,128)S(1)} %get-tuple-element.11.refs_0_, f32[96,768]{1,0:T(8,128)S(1)} %get-tuple-element.12.refs_1_, f32[96,768]{1,0:T(8,128)S(1)} %get-tuple-element.13.refs_2_), custom_call_target="tpu_custom_call" | custom-call | tf_op jit(solution)/shard_map/pallas_call | solution.py:515
Async XLA Ops:
  0.6 0.7 copy-start

commit v6 on v5

--- a/solution.py
+++ b/solution.py
@@ -31,9 +31,9 @@
     (LAST, (0, 1), 2, 34.6, (42.4, 46.2, 54)),
     (LAST, (1, 0), 2, 34.7, (42.5, 46.3, 54.1)),
     (FIRST, (2,), 5, 18.8, (36.2, 50)),
-    (FIRST, (2,), 5, 25.9, (38.7, 50.1)),
+    (FIRST, (2,), 6, 25.9, (38.7, 50.1)),
     (FIRST, (2,), 5, 27.8, (41.4, 51)),
-    (FIRST, (2,), 6, 29.6, (44.6, 52)),
+    (FIRST, (2,), 5, 29.6, (44.6, 52)),
     (MIDDLE, (1, 0), 1, 27, (30.8, 36, 49)),
     (MIDDLE, (0, 1), 1, 27.1, (30.9, 36.1, 49.1)),
     (MIDDLE, (1, 0), 2, 27.2, (35, 38.8, 50.5)),
@@ -266,6 +266,9 @@
         turn((nears[0][c], nears[1][c]), (relays[c], passes[c][0], passes[c][1]))
 
     arrivals[0].wait()
+    early = len(bands) - 1
+    ends = [piece[1] + piece[2] for piece in pieces if piece[0] == FIRST]
+    gone = 0
     for start in range(0, belief.shape[1], LANES * 3):
         value = belief_t[start : min(start + LANES * 3, in_width), :]
         if value.shape[0] < LANES * 3:
@@ -273,11 +276,12 @@
                 [value, jnp.zeros((LANES * 3 - value.shape[0], rows), jnp.bfloat16)], axis=0
             )
         belief[:, start : start + LANES * 3] = value.T
-    pl.semaphore_wait(barrier, len(partners))
-    early = len(bands) - 1
-    for c in range(early):
-        nears[0][c].start()
-        nears[1][c].start()
+        while gone < early and ends[gone] <= start + LANES * 3:
+            if gone == 0:
+                pl.semaphore_wait(barrier, len(partners))
+            nears[0][gone].start()
+            nears[1][gone].start()
+            gone += 1
     arrivals[2].wait()
     for c in range(0, own_hid, 256):
         value = jnp.dot(

time: 71.4 us -> 71.1 us (level)
  no operation moved by 1% of the time
where the time goes in v6:
time: 71.1 us; the launch traced here: 71 us
  Pallas kernels  69.7 us (98%)
    pallas_call x1, Pallas kernels, per_device(): pl.pallas_call(functools.partial(step_kernel, dims, params, pieces, shape...  68.7 us

profile of v6, /device:TPU:0, one launch (start us, length us, event | category | flops | bytes accessed | tf_op | source)
XLA Modules:
  0.0 71.0 jit_solution(889815354331792484)
XLA Ops:
  0.6 0.0 copy-start
  0.6 0.6 copy-done
  1.3 68.7 %shard_map.85 = (f32[48,2688]{1,0:T(8,128)S(1)}, f32[96,768]{1,0:T(8,128)S(1)}, f32[96,768]{1,0:T(8,128)S(1)}, f32[8,128]{1,0:T(8,128)S(1)}) custom-call(s32[2]{0:T(128)S(1)} %copy-done, bf16[2652,256]{1,0:T(8,128)(2,1)} %bitcast.6, bf16[1326,256]{1,0:T(8,128)(2,1)} %bitcast.7, bf16[2652,768]{1,0:T(8,128)(2,1)} %refs_3_.1, bf16[768,1536]{1,0:T(8,128)(2,1)} %refs_4_.1, ...), custom_call_target="tpu_custom_call" | custom-call | tf_op jit(solution)/shard_map/pallas_call | solution.py:459
  70.0 1.0 %shard_map.86 = (f32[48,2652]{1,0:T(8,128)}, f32[96,768]{1,0:T(8,128)}, f32[96,663]{1,0:T(8,128)}) custom-call(f32[8,128]{1,0:T(8,128)S(1)} %get-tuple-element.10.scale, f32[48,2688]{1,0:T(8,128)S(1)} %get-tuple-element.11.refs_0_, f32[96,768]{1,0:T(8,128)S(1)} %get-tuple-element.12.refs_1_, f32[96,768]{1,0:T(8,128)S(1)} %get-tuple-element.13.refs_2_), custom_call_target="tpu_custom_call" | custom-call | tf_op jit(solution)/shard_map/pallas_call | solution.py:519
Async XLA Ops:
  0.6 0.7 copy-start
